TPU v7x, 256 devices: a whole 4x4x8 slice. The times are simulated.
256 devices in a mesh: grid: 32 (over y, x, core), pair: 8 (over z).
Axes of the slice: x: 4, y: 4, z: 8, core: 2. Of those that a mesh axis runs over, the one named last changes fastest.
Arguments:
- orbitals: bfloat16 [64, 128, 4096], P('grid', None, 'pair'), may hold values from -6 to 6
- box_list: int32 [32, 8, 4], replicated, may hold values from 0 to 127, all different within a row
- pair_slots: int32 [32, 8, 4, 2], P('grid', 'pair'), may hold values from 0 to 3, as said below
- offsets: int32 [32, 8, 4, 3], P('grid', 'pair'), may hold values from -8 to 8
- pair_count: int32 [32, 8], P('grid', 'pair'), may hold values from 2 to 4, as said below
Outputs:
- exchange_field: float32 [64, 128, 4096], P('grid', None, 'pair')
Inputs may be any that keep to these rules, and one draw needn't show every extreme that they name: `box_list`: the 4 orbitals of one worker's list are all different. `pair_slots`: only the first pair_count entries of a worker's lists are used; the first 2 pairs of every worker name each slot of its list exactly once. `pair_count`: each group of 8 workers that share a grid index holds 24 pairs, and one of them holds 4.
All inputs are finite; a program needn't handle non-finite values.
Results may differ from a plain program's by a relative error of at most 0.0019.
Values may be sent and summed in bfloat16 or wider, within the bound.
A program may use at most 64 MiB of HBM per device.

v0:
```python
import math

import jax
import jax.numpy as jnp
from jax import lax
from jax.sharding import PartitionSpec as P

SHIFT = 8


screening = 0.02


def split_up(array, dim, size):
    shape = array.shape
    parts = array.reshape(*shape[:dim], size, shape[dim] // size, *shape[dim + 1 :])
    return jnp.moveaxis(parts, dim, 0)


def in_order(parts, dim):
    shape = list(parts.shape[1:])
    shape[dim] *= parts.shape[0]
    return jnp.moveaxis(parts, 0, dim).reshape(shape)


def joined_exchange(array, axis, axes, splits, concats):
    sizes = [lax.axis_size(a) for a in axes]
    parts = split_up(array, splits[0], sizes[0])
    parts = jnp.moveaxis(split_up(parts, splits[1] + 1, sizes[1]), 0, 1)
    inside = parts.shape[2:]
    parts = parts.reshape(-1, *inside)
    parts = lax.all_to_all(parts, axis, split_axis=0, concat_axis=0, tiled=True)
    parts = in_order(parts.reshape(*sizes, *inside), concats[0] + 1)
    return in_order(parts, concats[1])


def cas_table(extent):
    places = jnp.arange(extent, dtype=jnp.int32)
    product = places[:, None] * places[None, :] % extent
    phases = product.astype(jnp.float32) * (2.0 * math.pi / extent)
    return jnp.cos(phases) + jnp.sin(phases)


def green_table(extent):
    phases = jnp.arange(extent, dtype=jnp.int32).astype(jnp.float32) * (2.0 * math.pi / extent)
    eigen = 2.0 - 2.0 * jnp.cos(phases)
    denominator = screening + eigen[:, None, None] + eigen[None, :, None] + eigen[None, None, :]
    return 1.0 / (denominator * float(extent**3))


def poisson(density, table, green):
    high = lax.Precision.HIGHEST
    spectrum = jnp.einsum("ax,xyz->ayz", table, density, precision=high)
    spectrum = jnp.einsum("by,ayz->abz", table, spectrum, precision=high)
    spectrum = jnp.einsum("cz,abz->abc", table, spectrum, precision=high)
    spectrum = spectrum * green
    spectrum = jnp.einsum("ax,xyz->ayz", table, spectrum, precision=high)
    spectrum = jnp.einsum("by,ayz->abz", table, spectrum, precision=high)
    return jnp.einsum("cz,abz->abc", table, spectrum, precision=high)


def shift_box(field, step_x, step_y, step_z):
    extent = field.shape[0]
    padded = jnp.pad(field, SHIFT)
    starts = (SHIFT + step_x, SHIFT + step_y, SHIFT + step_z)
    return lax.dynamic_slice(padded, starts, (extent, extent, extent))


def worker_fields(box_data, slot_list, offset_list, pair_total):
    extent = box_data.shape[0]
    capacity = box_data.shape[1]
    table = cas_table(extent)
    green = green_table(extent)

    def fetch(slot):
        picked = lax.dynamic_index_in_dim(box_data, slot, 1, False)
        return picked.astype(jnp.float32).reshape(extent, extent, extent)

    def add_slot(collected, slot, value):
        current = lax.dynamic_index_in_dim(collected, slot, 1, True)
        updated = current + value.reshape(extent, 1, extent * extent)
        return lax.dynamic_update_index_in_dim(collected, updated, slot, 1)

    def one_pair(turn, collected):
        first_slot = slot_list[turn, 0]
        second_slot = slot_list[turn, 1]
        offset = offset_list[turn]
        first_box = fetch(first_slot)
        second_box = fetch(second_slot)
        shifted = shift_box(second_box, offset[0], offset[1], offset[2])
        potential = poisson(first_box * shifted, table, green)
        collected = add_slot(collected, first_slot, -(potential * shifted))
        returned = shift_box(-(potential * first_box), -offset[0], -offset[1], -offset[2])
        return add_slot(collected, second_slot, returned)

    start = jnp.zeros((extent, capacity, extent * extent), jnp.float32)
    collected = lax.fori_loop(jnp.int32(0), pair_total, one_pair, start)
    return collected.astype(jnp.bfloat16)


def shards(orbitals, box_list, pair_slots, offsets, pair_count):
    planes, orbital_total, row_cells = orbitals.shape
    grid_count, pair_workers, capacity = box_list.shape
    extent = planes * grid_count
    routing = jnp.transpose(box_list, (0, 2, 1)).reshape(-1)
    outgoing = jnp.take(orbitals, routing, axis=1)
    outgoing = outgoing.reshape(planes, grid_count, capacity, pair_workers, row_cells)
    arrived = joined_exchange(outgoing, ("grid", "pair"), ("grid", "pair"), (1, 3), (0, 4))
    box_data = arrived.reshape(extent, capacity, extent * extent)
    fields = worker_fields(box_data, pair_slots[0, 0], offsets[0, 0], pair_count[0, 0])
    outbound = fields.reshape(extent, 1, capacity, 1, extent * extent)
    landed = joined_exchange(outbound, ("grid", "pair"), ("grid", "pair"), (0, 4), (1, 3))
    pieces = jnp.moveaxis(landed.reshape(planes, -1, row_cells), 1, 0)
    summed = jax.ops.segment_sum(pieces.astype(jnp.float32), routing, num_segments=orbital_total)
    return jnp.moveaxis(summed, 0, 1)


def solution(mesh):
    placed = (
        P("grid", None, "pair"),
        P(),
        P("grid", "pair", None, None),
        P("grid", "pair", None, None),
        P("grid", "pair"),
    )
    return jax.shard_map(
        shards, mesh=mesh, in_specs=placed, out_specs=P("grid", None, "pair"), check_vma=False
    )
```

profile of v0, /device:TPU:1, one launch (start us, length us, event | category | flops | bytes accessed | tf_op | source)
XLA Modules:
  0.0 540.5 jit_solution(420208115465007898)
XLA Ops:
  1.9 8.4 %gather_fusion = bf16[1024,2,512]{2,0,1:T(8,128)(2,1)S(1)} fusion(bf16[2,128,512]{2,1,0:T(8,128)(2,1)S(1)} %copy-done, s32[1024]{0:T(1024)S(1)} %broadcast_clamp_fusion), kind=kCustom, calls=%fused_computation | custom fusion | bytes 4198400 | tf_op jit(solution)/shard_map/jit(_take)/gather | solution.py:106
  10.6 3.0 copy.42
  13.5 15.6 %all-to-all-start = ((bf16[256,2,1,4,1,512]{5,3,1,4,2,0:T(4,128)(2,1)}), bf16[256,2,1,4,1,512]{5,3,1,4,2,0:T(4,128)(2,1)S(1)}, u32[]{:S(2)}, u32[]{:S(2)}) async-start(bf16[256,2,1,4,1,512]{5,3,1,4,2,0:T(4,128)(2,1)} %copy.42), calls=%async_computation | async-start | bytes 4194304 | tf_op jit(solution)/shard_map/all_to_all | solution.py:32
  29.4 53.7 %all-to-all-done = bf16[256,2,1,4,1,512]{5,3,1,4,2,0:T(4,128)(2,1)S(1)} async-done(((bf16[256,2,1,4,1,512]{5,3,1,4,2,0:T(4,128)(2,1)}), bf16[256,2,1,4,1,512]{5,3,1,4,2,0:T(4,128)(2,1)S(1)}, u32[]{:S(2)}, u32[]{:S(2)}) %all-to-all-start) | async-done | bytes 2097184 | tf_op jit(solution)/shard_map/all_to_all | solution.py:32
  84.1 2.8 reshape_reshape.2
  86.9 4.1 copy.46
  93.4 291.5 %while.15 = (s32[]{:T(128)}, f32[64,4,4096]{2,0,1:T(8,128)}, s32[]{:T(128)}, s32[4,2]{0,1:T(2,128)S(1)}, bf16[64,4,4096]{2,0,1:T(8,128)(2,1)}, /*index=5*/s32[4,...) while((s32[]{:T(128)}, f32[64,4,4096]{2,0,1:T(8,128)}, ...), condition=%wide.region_1.2_spmd.clone.clone, body=%wide.region_0.1_spmd.clone.clone.sunk | while | flops 1211998208 | bytes 44581792 | solution.py:97
  128.0 5.7 %fusion.90 = f32[64,64,64]{0,2,1:T(8,128)} fusion(f32[64,64,64]{2,1,0:T(8,128)S(1)} %convert_multiply_fusion.3), kind=kOutput, calls=%fused_computation.19.clone.1 | convolution fusion | flops 201388032 | bytes 2097152 | tf_op jit(solution)/shard_map/while/body/ax,xyz->ayz/dot_general | solution.py:53
  133.7 4.2 copy.78
  137.9 3.6 fusion.91
  141.5 3.9 divide_multiply_fusion.2
  145.4 5.7 %fusion.92 = f32[64,64,64]{0,2,1:T(8,128)} fusion(f32[64,64,64]{2,1,0:T(8,128)S(1)} %divide_multiply_fusion.2), kind=kOutput, calls=%fused_computation.20.clone.1 | convolution fusion | flops 201388032 | bytes 2097152 | tf_op jit(solution)/shard_map/while/body/ax,xyz->ayz/dot_general | solution.py:57
  151.1 4.2 copy.79
  155.3 3.6 fusion.93
  158.9 6.1 %multiply_negate_fusion.2 = (f32[64,64,64]{2,1,0:T(8,128)}, f32[64,64,64]{2,1,0:T(8,128)}) fusion(f32[64,64,64]{2,1,0:T(8,128)S(1)} %reshape.227, s32[]{:T(128)S(6)} %select_n.205, s32[]{:T(128)S(6)} %select_n.206, s32[]{:T(128)S(6)} %select_n.207, bf16[64,64,64]{2,1,0:T(8,128)(2,1)S(1)} %convert_element_type.143, f32[64,64,64]{2,1,0:T(8,128)S(1)} %fusion.93), kind=kOutput, calls=%fused_computation.17.clone.1 | convolution fusion | flops 202698752 | bytes 4718604 | tf_op jit(solution)/shard_map/while/body/cz,abz->abc/dot_general | solution.py:59
  167.0 2.5 add_dynamic-update-slice_fusion.4
  171.4 2.5 pad_dynamic-slice_fusion.3
  194.3 5.7 %fusion.90 = f32[64,64,64]{0,2,1:T(8,128)} fusion(f32[64,64,64]{2,1,0:T(8,128)S(1)} %convert_multiply_fusion.3), kind=kOutput, calls=%fused_computation.19.clone.1 | convolution fusion | flops 201388032 | bytes 2097152 | tf_op jit(solution)/shard_map/while/body/ax,xyz->ayz/dot_general | solution.py:53
  200.0 4.2 copy.78
  204.1 3.6 fusion.91
  207.7 3.9 divide_multiply_fusion.2
  211.7 5.7 %fusion.92 = f32[64,64,64]{0,2,1:T(8,128)} fusion(f32[64,64,64]{2,1,0:T(8,128)S(1)} %divide_multiply_fusion.2), kind=kOutput, calls=%fused_computation.20.clone.1 | convolution fusion | flops 201388032 | bytes 2097152 | tf_op jit(solution)/shard_map/while/body/ax,xyz->ayz/dot_general | solution.py:57
  217.4 4.2 copy.79
  221.5 3.6 fusion.93
  225.1 6.1 %multiply_negate_fusion.2 = (f32[64,64,64]{2,1,0:T(8,128)}, f32[64,64,64]{2,1,0:T(8,128)}) fusion(f32[64,64,64]{2,1,0:T(8,128)S(1)} %reshape.227, s32[]{:T(128)S(6)} %select_n.205, s32[]{:T(128)S(6)} %select_n.206, s32[]{:T(128)S(6)} %select_n.207, bf16[64,64,64]{2,1,0:T(8,128)(2,1)S(1)} %convert_element_type.143, f32[64,64,64]{2,1,0:T(8,128)S(1)} %fusion.93), kind=kOutput, calls=%fused_computation.17.clone.1 | convolution fusion | flops 202698752 | bytes 4718604 | tf_op jit(solution)/shard_map/while/body/cz,abz->abc/dot_general | solution.py:59
  237.6 2.5 pad_dynamic-slice_fusion.3
  260.5 5.7 %fusion.90 = f32[64,64,64]{0,2,1:T(8,128)} fusion(f32[64,64,64]{2,1,0:T(8,128)S(1)} %convert_multiply_fusion.3), kind=kOutput, calls=%fused_computation.19.clone.1 | convolution fusion | flops 201388032 | bytes 2097152 | tf_op jit(solution)/shard_map/while/body/ax,xyz->ayz/dot_general | solution.py:53
  266.2 4.2 copy.78
  270.4 3.6 fusion.91
  274.0 3.9 divide_multiply_fusion.2
  277.9 5.7 %fusion.92 = f32[64,64,64]{0,2,1:T(8,128)} fusion(f32[64,64,64]{2,1,0:T(8,128)S(1)} %divide_multiply_fusion.2), kind=kOutput, calls=%fused_computation.20.clone.1 | convolution fusion | flops 201388032 | bytes 2097152 | tf_op jit(solution)/shard_map/while/body/ax,xyz->ayz/dot_general | solution.py:57
  283.6 4.2 copy.79
  287.7 3.6 fusion.93
  291.3 6.1 %multiply_negate_fusion.2 = (f32[64,64,64]{2,1,0:T(8,128)}, f32[64,64,64]{2,1,0:T(8,128)}) fusion(f32[64,64,64]{2,1,0:T(8,128)S(1)} %reshape.227, s32[]{:T(128)S(6)} %select_n.205, s32[]{:T(128)S(6)} %select_n.206, s32[]{:T(128)S(6)} %select_n.207, bf16[64,64,64]{2,1,0:T(8,128)(2,1)S(1)} %convert_element_type.143, f32[64,64,64]{2,1,0:T(8,128)S(1)} %fusion.93), kind=kOutput, calls=%fused_computation.17.clone.1 | convolution fusion | flops 202698752 | bytes 4718604 | tf_op jit(solution)/shard_map/while/body/cz,abz->abc/dot_general | solution.py:59
  299.5 2.5 add_dynamic-update-slice_fusion.4
  326.7 5.7 %fusion.90 = f32[64,64,64]{0,2,1:T(8,128)} fusion(f32[64,64,64]{2,1,0:T(8,128)S(1)} %convert_multiply_fusion.3), kind=kOutput, calls=%fused_computation.19.clone.1 | convolution fusion | flops 201388032 | bytes 2097152 | tf_op jit(solution)/shard_map/while/body/ax,xyz->ayz/dot_general | solution.py:53
  332.4 4.2 copy.78
  336.6 3.6 fusion.91
  340.2 3.9 divide_multiply_fusion.2
  344.1 5.7 %fusion.92 = f32[64,64,64]{0,2,1:T(8,128)} fusion(f32[64,64,64]{2,1,0:T(8,128)S(1)} %divide_multiply_fusion.2), kind=kOutput, calls=%fused_computation.20.clone.1 | convolution fusion | flops 201388032 | bytes 2097152 | tf_op jit(solution)/shard_map/while/body/ax,xyz->ayz/dot_general | solution.py:57
  349.8 4.2 copy.79
  354.0 3.6 fusion.93
  357.6 6.1 %multiply_negate_fusion.2 = (f32[64,64,64]{2,1,0:T(8,128)}, f32[64,64,64]{2,1,0:T(8,128)}) fusion(f32[64,64,64]{2,1,0:T(8,128)S(1)} %reshape.227, s32[]{:T(128)S(6)} %select_n.205, s32[]{:T(128)S(6)} %select_n.206, s32[]{:T(128)S(6)} %select_n.207, bf16[64,64,64]{2,1,0:T(8,128)(2,1)S(1)} %convert_element_type.143, f32[64,64,64]{2,1,0:T(8,128)S(1)} %fusion.93), kind=kOutput, calls=%fused_computation.17.clone.1 | convolution fusion | flops 202698752 | bytes 4718604 | tf_op jit(solution)/shard_map/while/body/cz,abz->abc/dot_general | solution.py:59
  388.5 3.0 copy.48
  391.4 6.4 %all-to-all-start.1 = ((bf16[256,2,1,4,1,512]{5,3,1,4,2,0:T(4,128)(2,1)}), bf16[256,2,1,4,1,512]{5,3,1,4,2,0:T(4,128)(2,1)S(1)}, u32[]{:S(2)}, u32[]{:S(2)}) async-start(bf16[256,2,1,4,1,512]{5,3,1,4,2,0:T(4,128)(2,1)} %copy.48), calls=%async_computation.1 | async-start | bytes 4194304 | tf_op jit(solution)/shard_map/all_to_all | solution.py:32
  397.9 53.9 %all-to-all-done.1 = bf16[256,2,1,4,1,512]{5,3,1,4,2,0:T(4,128)(2,1)S(1)} async-done(((bf16[256,2,1,4,1,512]{5,3,1,4,2,0:T(4,128)(2,1)}), bf16[256,2,1,4,1,512]{5,3,1,4,2,0:T(4,128)(2,1)S(1)}, u32[]{:S(2)}, u32[]{:S(2)}) %all-to-all-start.1) | async-done | bytes 2097184 | tf_op jit(solution)/shard_map/all_to_all | solution.py:32
  453.0 5.2 copy.51
  458.3 81.1 %scatter_fusion = f32[128,2,512]{2,1,0:T(2,128)S(1)} fusion(f32[128,2,512]{2,1,0:T(2,128)S(1)} %broadcast_in_dim.21, s32[1024]{0:T(1024)S(1)} %reshape.212, f32[1024,2,512]{2,1,0:T(2,128)} %copy.51), kind=kCustom, calls=%fused_computation.1 | custom fusion | flops 1048576 | bytes 12587008 | tf_op jit(solution)/shard_map/scatter-add | solution.py:114
  (81 shorter events, 78.5 us)
Async XLA Ops:
  0.0 1.9 copy-start
  13.5 15.7 %copy-start.4 = (s32[1,1,4,3]{2,1,3,0:T(1,128)S(1)}, s32[1,1,4,3]{2,1,3,0:T(1,128)}, u32[]{:S(2)}) copy-start(s32[1,1,4,3]{2,1,3,0:T(1,128)} %param.10) | copy-start | bytes 148
  13.5 69.6 %all-to-all-start = ((bf16[256,2,1,4,1,512]{5,3,1,4,2,0:T(4,128)(2,1)}), bf16[256,2,1,4,1,512]{5,3,1,4,2,0:T(4,128)(2,1)S(1)}, u32[]{:S(2)}, u32[]{:S(2)}) async-start(bf16[256,2,1,4,1,512]{5,3,1,4,2,0:T(4,128)(2,1)} %copy.42), calls=%async_computation | async-start | bytes 4194304 | tf_op jit(solution)/shard_map/all_to_all | solution.py:32
  90.9 2.4 copy-start.3
  167.0 4.4 copy-start.2
  233.3 4.3 copy-start.2
  299.5 4.4 copy-start.2
  365.7 4.3 copy-start.2
  391.4 60.4 %all-to-all-start.1 = ((bf16[256,2,1,4,1,512]{5,3,1,4,2,0:T(4,128)(2,1)}), bf16[256,2,1,4,1,512]{5,3,1,4,2,0:T(4,128)(2,1)S(1)}, u32[]{:S(2)}, u32[]{:S(2)}) async-start(bf16[256,2,1,4,1,512]{5,3,1,4,2,0:T(4,128)(2,1)} %copy.48), calls=%async_computation.1 | async-start | bytes 4194304 | tf_op jit(solution)/shard_map/all_to_all | solution.py:32
  458.3 82.0 %copy-start.1 = (bf16[2,128,512]{2,1,0:T(8,128)(2,1)S(1)}, bf16[2,128,512]{2,1,0:T(8,128)(2,1)}, u32[]{:S(2)}) copy-start(bf16[2,128,512]{2,1,0:T(8,128)(2,1)} %param.7) | copy-start | bytes 786436
where the time goes:
time: 550 us; the launch traced here: 541 us
  other arithmetic  119 us (22%)
  matrix products  114 us (21%)
  local copies, waits for them, and re-layouts  110 us (20%)
  waiting for transfers between devices  108 us (20%)
  loops' own time  67.2 us (12%)
  starting transfers between devices  22 us (4%)
    all_to_all x2, waiting for transfers between devices, joined_exchange(): parts = lax.all_to_all(parts, axis, split_axis=0, concat_axis=0, tiled=True)  108 us
    scatter-add x1, other arithmetic, shards(): jax.ops.segment_sum(pieces.astype(jnp.float32), routing, num_segments=orb...  81.1 us
    another operation x1, loops' own time, worker_fields(): collected = lax.fori_loop(jnp.int32(0), pair_total, one_pair, start)  67.2 us
    dot_general x8, matrix products, poisson(): spectrum = jnp.einsum('by,ayz->abz', table, spectrum, precision=high)  28.7 us
    dot_general x4, matrix products, poisson(): return jnp.einsum('cz,abz->abc', table, spectrum, precision=high)  24.2 us
    dot_general x4, matrix products, poisson(): spectrum = jnp.einsum('ax,xyz->ayz', table, spectrum, precision=high)  22.8 us
    dot_general x4, matrix products, poisson(): spectrum = jnp.einsum('ax,xyz->ayz', table, density, precision=high)  22.8 us
    all_to_all x2, starting transfers between devices, joined_exchange(): parts = lax.all_to_all(parts, axis, split_axis=0, concat_axis=0, tiled=True)  22 us
  transfers between devices with their start and end apart: 2, of which 2 were waited for; matrix products, arithmetic and copies ran while one was open for 0% of the time, Pallas kernels for 0%

commit v1 on v0

v1 whole, which is shorter than its diff:
```python
import math
import numpy as np
import jax
import jax.numpy as jnp
from jax import lax
from jax.experimental import pallas as pl
from jax.experimental.pallas import tpu as pltpu
from jax.sharding import PartitionSpec as P

screening = 0.02
N = 64
CH = 16
W = 256
PITCH = 72
f32, bf16 = jnp.float32, jnp.bfloat16


def tables():
    m = np.arange(N)
    ph = 2.0 * math.pi * ((m[:, None] * m[None, :]) % N) / N
    cas = np.cos(ph) + np.sin(ph)
    perm = np.concatenate([np.arange(0, N, 2), np.arange(1, N, 2)])

    def parts(a):
        a = np.asarray(a, np.float32)
        hi = a.astype(bf16)
        lo = (a - hi.astype(np.float32)).astype(bf16)
        return hi, lo

    def left(a):
        hi, lo = parts(a)
        return np.concatenate([hi, hi, lo], axis=1)

    cx = left(cas)
    cf = left(cas[:, perm])
    ci = left(cas[perm, :])
    hi, lo = parts(np.kron(np.eye(4), cas))
    bd = np.concatenate([hi, hi, lo], axis=0)
    e = 2.0 - 2.0 * np.cos(2.0 * math.pi * m / N)
    green = 1.0 / ((screening + e[:, None, None] + e[None, :, None] + e[None, None, :]) * float(N**3))
    g = green.reshape(CH, 4, N, N).transpose(0, 2, 1, 3).reshape(CH, N, W).astype(np.float32)
    return cx, cf, ci, bd, g


def split(v):
    hi = v.astype(bf16)
    lo = (v - hi.astype(f32)).astype(bf16)
    return hi, lo


def mm(a, b):
    return jnp.dot(a, b, preferred_element_type=f32)


def left_mul(table, v):
    hi, lo = split(v)
    return mm(table, jnp.concatenate([hi, lo, hi], axis=0))


def right_mul(v, bd):
    hi, lo = split(v)
    return mm(jnp.concatenate([hi, lo, hi], axis=1), bd)


def pair_kernel(slots, offs, count, box, cx, cf, ci, bd, green, out, pad, sh, U, wh, wl, col):
    GR = 4
    low = lax.broadcasted_iota(jnp.int32, (32, 128), 1) < 64
    zpad = jnp.zeros((4, N, W), bf16)
    for r in (pad, wh, wl):
        r[0:4] = zpad
        r[20:24] = zpad
    col[...] = jnp.zeros(col.shape, f32)

    def pair(k, carry):
        a = slots[k, 0]
        b = slots[k, 1]
        dx, dy, dz = offs[k, 0], offs[k, 1], offs[k, 2]
        t = dy * 64 + dz
        q = (t + 1024) // 256 - 4
        r = t - 256 * q
        rows = lax.broadcasted_iota(jnp.int32, (W, W), 0)
        cols = lax.broadcasted_iota(jnp.int32, (W, W), 1)
        zc = cols % 64 + dz
        okc = (zc >= 0) & (zc < 64)
        one, zero = jnp.float32(1), jnp.float32(0)

        def mask(c):
            return jnp.where(c, one, zero).astype(bf16)

        fwd = jnp.concatenate([mask(okc & (rows == cols + r)), mask(okc & (rows == cols + r - 256))], axis=0)
        zr = rows % 64 + dz
        okr = (zr >= 0) & (zr < 64)
        b0 = mask(okr & (cols == rows + r))
        b1 = mask(okr & (cols == rows + r - 256))
        bwd = jnp.concatenate([b0, b0, b1, b1], axis=0)
        xr = lax.broadcasted_iota(jnp.int32, (N, N), 0)
        xc = lax.broadcasted_iota(jnp.int32, (N, N), 1)
        sx = mask(xc == xr + dx)
        sxt = mask(xr == xc + dx)

        pad[4:20] = box[b]

        def forward(g, c):
            lo_ = g * GR
            src0 = pad[pl.ds(lo_ + 4 + q, GR)].reshape(GR * N, W)
            src1 = pad[pl.ds(lo_ + 5 + q, GR)].reshape(GR * N, W)
            yz = mm(jnp.concatenate([src0, src1], axis=1), fwd).astype(bf16).reshape(GR, N, W)
            outs = []
            for i in range(GR):
                s = mm(sx, yz[i])
                sh[lo_ + i] = s.astype(bf16)
                dens = box[a, lo_ + i].astype(f32) * s
                outs.append(left_mul(cx[...], dens))
            spec = right_mul(jnp.concatenate(outs, axis=0), bd[...])
            for i in range(GR):
                for h in range(2):
                    U[pl.ds(pl.multiple_of((2 * (lo_ + i) + h) * PITCH, 8), N), :] = spec[i * N:(i + 1) * N, h * 128:(h + 1) * 128]
            return c

        lax.fori_loop(0, CH // GR, forward, 0)

        def middle(g, c):
            tops, bots = [], []
            for h in range(2):
                l1 = U[pl.ds(g * 4 + 2 * h, 32, stride=PITCH), :]
                l2 = U[pl.ds(g * 4 + 2 * h + 1, 32, stride=PITCH), :]
                tops.append(jnp.where(low, l1, pltpu.roll(l2, 64, 1)))
                bots.append(jnp.where(low, pltpu.roll(l1, 64, 1), l2))
            v = jnp.concatenate([jnp.concatenate(tops, axis=1), jnp.concatenate(bots, axis=1)], axis=0)
            s = left_mul(cf[...], v) * green[g]
            p = left_mul(ci[...], s)
            for h in range(2):
                x0 = p[:32, h * 128:(h + 1) * 128]
                x1 = p[32:, h * 128:(h + 1) * 128]
                U[pl.ds(g * 4 + 2 * h, 32, stride=PITCH), :] = jnp.where(low, x0, pltpu.roll(x1, 64, 1))
                U[pl.ds(g * 4 + 2 * h + 1, 32, stride=PITCH), :] = jnp.where(low, pltpu.roll(x0, 64, 1), x1)
            return c

        lax.fori_loop(0, CH, middle, 0)

        def inverse(g, c):
            lo_ = g * GR
            outs = []
            for i in range(GR):
                v = jnp.concatenate(
                    [U[pl.ds(pl.multiple_of((2 * (lo_ + i) + h) * PITCH, 8), N), :] for h in range(2)], axis=1)
                outs.append(left_mul(cx[...], v))
            pot = right_mul(jnp.concatenate(outs, axis=0), bd[...]).reshape(GR, N, W)
            for i in range(GR):
                j = lo_ + i
                col[a, j] = col[a, j] - pot[i] * sh[j].astype(f32)
                hi, lo = split(-(pot[i] * box[a, j].astype(f32)))
                wh[j + 4] = mm(sxt, hi).astype(bf16)
                wl[j + 4] = mm(sxt, lo).astype(bf16)
            return c

        lax.fori_loop(0, CH // GR, inverse, 0)

        def back(g, c):
            lo_ = g * GR
            i0 = lo_ + 4 - q
            parts_ = [r_[pl.ds(i, GR)].reshape(GR * N, W) for i in (i0, i0 - 1) for r_ in (wh, wl)]
            u = mm(jnp.concatenate(parts_, axis=1), bwd)
            col[b, pl.ds(lo_, GR)] = col[b, pl.ds(lo_, GR)] + u.reshape(GR, N, W)
            return c

        lax.fori_loop(0, CH // GR, back, 0)
        return carry

    lax.fori_loop(0, count[0], pair, 0)
    out[...] = col[...].astype(bf16)


def worker_fields(box, slots, offs, count):
    cx, cf, ci, bd, g = (jnp.asarray(t) for t in tables())
    smem = pl.BlockSpec(memory_space=pltpu.SMEM)
    vmem = pl.BlockSpec(memory_space=pltpu.VMEM)
    return pl.pallas_call(
        pair_kernel,
        out_shape=jax.ShapeDtypeStruct((4, CH, N, W), bf16),
        in_specs=[smem] * 3 + [vmem] * 6,
        out_specs=vmem,
        scratch_shapes=[
            pltpu.VMEM((24, N, W), bf16),
            pltpu.VMEM((CH, N, W), bf16),
            pltpu.VMEM((32 * PITCH, 128), f32),
            pltpu.VMEM((24, N, W), bf16),
            pltpu.VMEM((24, N, W), bf16),
            pltpu.VMEM((4, CH, N, W), f32),
        ],
        compiler_params=pltpu.CompilerParams(vmem_limit_bytes=40 << 20),
        name="pairs",
    )(slots, offs, count, box, cx, cf, ci, bd, g)


def shards(orbitals, box_list, pair_slots, offsets, pair_count):
    planes, orbital_total, row_cells = orbitals.shape
    lists = box_list.reshape(-1)
    hot = (lists[:, None] == jnp.arange(orbital_total, dtype=jnp.int32)[None, :]).astype(bf16)
    local = orbitals.reshape(planes, orbital_total, 2, W)
    picked = jnp.einsum("ro,xojc->rjxc", hot, local, preferred_element_type=f32).astype(bf16)
    picked = picked.reshape(256, 4, 2, planes, W)
    arrived = lax.all_to_all(picked, ("grid", "pair"), split_axis=0, concat_axis=0, tiled=True)
    box = arrived.reshape(32, 8, 4, 2, planes, W).transpose(2, 1, 3, 0, 4, 5).reshape(4, CH, N, W)
    fields = worker_fields(box, pair_slots[0, 0], offsets[0, 0], pair_count[0])
    back = fields.reshape(4, 8, 2, 32, planes, W).transpose(3, 1, 0, 2, 4, 5).reshape(256, 4, 2, planes, W)
    landed = lax.all_to_all(back, ("grid", "pair"), split_axis=0, concat_axis=0, tiled=True)
    landed = landed.reshape(1024, 2, planes, W)
    summed = jnp.einsum("ro,rjxc->xojc", hot, landed, preferred_element_type=f32)
    return summed.reshape(planes, orbital_total, row_cells)


def solution(mesh):
    placed = (
        P("grid", None, "pair"),
        P(),
        P("grid", "pair", None, None),
        P("grid", "pair", None, None),
        P("grid", "pair"),
    )
    return jax.shard_map(
        shards, mesh=mesh, in_specs=placed, out_specs=P("grid", None, "pair"), check_vma=False
    )
```

time: 550 us -> 221 us (0.40); the launches traced: 541 us -> 220 us
  other arithmetic: 119 us -> 0 us
  matrix products: 114 us -> 2.66 us
  local copies, waits for them, and re-layouts: 110 us -> 22.6 us
  blocking collectives: 0 us -> 75.3 us
  loops' own time: 67.2 us -> 0 us
  waiting for transfers between devices: 108 us -> 53 us
  Pallas kernels: 0 us -> 50.2 us
  starting transfers between devices: 22 us -> 15.6 us
    dot_general x24 -> x2, matrix products: 114 us -> 2.66 us  [the longest x1 1.7 us: shards(): jnp.einsum('ro,xojc->rjxc', hot, local, preferred_element_type=f32)]
    scatter-add x1 -> x0, other arithmetic: 81.1 us -> none  [shards(): jax.ops.segment_sum(pieces.astype(jnp.float32), routing, num_segments=orb...]
    all_to_all x0 -> x1, blocking collectives: none -> 75.3 us  [shards(): lax.all_to_all(back, ('grid', 'pair'), split_axis=0, concat_axis=0, tiled...]
    another operation x1 -> x0, loops' own time: 67.2 us -> none  [worker_fields(): collected = lax.fori_loop(jnp.int32(0), pair_total, one_pair, start)]
    all_to_all x2 -> x1, waiting for transfers between devices: 108 us -> 53 us  [shards(): lax.all_to_all(picked, ('grid', 'pair'), split_axis=0, concat_axis=0, til...]
    pallas_call x0 -> x1, Pallas kernels: none -> 50.2 us  [worker_fields(): pl.pallas_call(pair_kernel, out_shape=jax.ShapeDtypeStruct((4, CH, N, W),...]
    dot_general x8 -> x0, local copies, waits for them, and re-layouts: 33.2 us -> none  [the longest x4 16.6 us: poisson(): spectrum = jnp.einsum('ax,xyz->ayz', table, density, precision=high)]
    dynamic_update_slice x8 -> x0, other arithmetic: 19.2 us -> none  [add_slot(): return lax.dynamic_update_index_in_dim(collected, updated, slot, 1)]
  transfers between devices with their start and end apart: 2 -> 1, of which waited for: 2 -> 1; matrix products, arithmetic and copies ran while one was open for 0% -> 0% of each run, Pallas kernels for 0% -> 0%
where the time goes in v1:
time: 221 us; the launch traced here: 220 us
  blocking collectives  75.3 us (34%)
  waiting for transfers between devices  53 us (24%)
  Pallas kernels  50.2 us (23%)
  local copies, waits for them, and re-layouts  22.6 us (10%)
  starting transfers between devices  15.6 us (7%)
  matrix products  2.66 us (1%)
    all_to_all x1, blocking collectives, shards(): lax.all_to_all(back, ('grid', 'pair'), split_axis=0, concat_axis=0, tiled...  75.3 us
    all_to_all x1, waiting for transfers between devices, shards(): lax.all_to_all(picked, ('grid', 'pair'), split_axis=0, concat_axis=0, til...  53 us
    pallas_call x1, Pallas kernels, worker_fields(): pl.pallas_call(pair_kernel, out_shape=jax.ShapeDtypeStruct((4, CH, N, W),...  50.2 us
    all_to_all x1, starting transfers between devices, shards(): lax.all_to_all(picked, ('grid', 'pair'), split_axis=0, concat_axis=0, til...  15.6 us
    reshape x3, local copies, waits for them, and re-layouts, shards(): fields.reshape(4, 8, 2, 32, planes, W).transpose(3, 1, 0, 2, 4, 5)  6.17 us
    unnamed x18, local copies, waits for them, and re-layouts  4.56 us
  transfers between devices with their start and end apart: 1, of which 1 were waited for; matrix products, arithmetic and copies ran while one was open for 0% of the time, Pallas kernels for 0%

profile of v1, /device:TPU:1, one launch (start us, length us, event | category | flops | bytes accessed | tf_op | source)
XLA Modules:
  0.0 220.2 jit_solution(3734561035476885605)
XLA Ops:
  0.0 0.9 copy.26
  0.9 0.1 eq.15
  1.0 1.7 convert_bitcast_fusion
  2.7 3.5 %copy.38 = bf16[1024,2,2,256]{3,2,1,0:T(2,128)(2,1)} copy(bf16[1024,2,2,256]{3,0,1,2:T(8,128)(2,1)S(1)} %convert_bitcast_fusion) | data formatting | bytes 4194304 | tf_op jit(solution)/shard_map/reshape | solution.py:202
  6.2 0.0 copy-start.6
  6.2 0.0 copy-start.7
  6.2 15.6 %all-to-all-start = ((bf16[256,4,2,2,256]{4,3,2,1,0:T(2,128)(2,1)}), bf16[256,4,2,2,256]{4,3,2,1,0:T(2,128)(2,1)S(1)}, u32[]{:S(2)}, u32[]{:S(2)}) async-start(bf16[256,4,2,2,256]{4,3,2,1,0:T(2,128)(2,1)} %bitcast.34), calls=%async_computation | async-start | bytes 4194304 | tf_op jit(solution)/shard_map/all_to_all | solution.py:203
  21.8 0.0 copy-done.6
  21.8 0.1 copy.25
  21.9 0.0 copy-done.7
  21.9 0.1 copy.31.slots
  22.7 53.0 %all-to-all-done = bf16[256,4,2,2,256]{4,3,2,1,0:T(2,128)(2,1)S(1)} async-done(((bf16[256,4,2,2,256]{4,3,2,1,0:T(2,128)(2,1)}), bf16[256,4,2,2,256]{4,3,2,1,0:T(2,128)(2,1)S(1)}, u32[]{:S(2)}, u32[]{:S(2)}) %all-to-all-start) | async-done | bytes 2097184 | tf_op jit(solution)/shard_map/all_to_all | solution.py:203
  75.7 0.7 copy.51
  76.4 3.5 %copy.30 = bf16[4,8,2,32,2,256]{5,4,3,2,1,0:T(2,128)(2,1)} copy(bf16[4,8,2,32,2,256]{5,1,3,4,2,0:T(8,128)(2,1)S(1)} %bitcast.35) | data formatting | bytes 4194304 | tf_op jit(solution)/shard_map/transpose | solution.py:204
  80.0 0.0 copy-start.1
  80.0 0.0 copy-start.2
  80.0 2.9 %reshape.28.box = bf16[4,16,64,256]{3,2,1,0:T(8,128)(2,1)S(1)} reshape(bf16[4,8,2,32,2,256]{5,4,3,2,1,0:T(2,128)(2,1)} %copy.30) | data formatting | bytes 4194304 | tf_op jit(solution)/shard_map/reshape | solution.py:204
  82.8 0.0 copy-done.1
  82.8 0.0 copy-done.2
  82.9 0.0 copy-start.3
  82.9 0.7 copy-done.3
  83.6 0.0 copy-start.4
  83.6 0.8 copy-done.4
  84.4 0.0 copy-start.5
  84.4 0.8 copy-done.5
  85.1 50.2 %pairs.1 = bf16[4,16,64,256]{3,2,1,0:T(8,128)(2,1)S(1)} custom-call(s32[4,2]{1,0:T(4,128)S(1)} %copy.31.slots, s32[4,3]{1,0:T(4,128)S(1)} %bitcast.33, s32[1]{0:T(128)} %bitcast.32.count, bf16[4,16,64,256]{3,2,1,0:T(8,128)(2,1)S(1)} %reshape.28.box, bf16[64,192]{1,0:T(8,128)(2,1)S(1)} %copy-done.3, bf16[64,192]{1,0:T(8,128)(2,1)S(1)} %copy-done.4, ...), custom_call_target="tpu_custom_call" | custom-call | tf_op jit(solution)/shard_map/pairs/pallas_call | solution.py:178
  135.3 0.0 copy-start
  135.3 1.3 copy-done
  136.7 2.7 %reshape.29 = bf16[4,8,2,32,2,256]{5,4,3,2,1,0:T(2,128)(2,1)S(1)} reshape(bf16[4,16,64,256]{3,2,1,0:T(8,128)(2,1)} %copy-done) | data formatting | bytes 4194304 | tf_op jit(solution)/shard_map/reshape | solution.py:206
  139.4 1.3 copy.50
  140.7 2.2 copy.33
  142.9 75.3 %all_to_all.10 = bf16[256,4,2,2,256]{4,3,2,1,0:T(2,128)(2,1)S(1)} all-to-all(bf16[256,4,2,2,256]{4,3,2,1,0:T(2,128)(2,1)S(1)} %copy.33), channel_id=1, replica_groups=mesh['grid'=32,'pair'=8] {'grid','pair'}, dimensions={0} | all-to-all | bytes 4194304 | tf_op jit(solution)/shard_map/all_to_all | solution.py:207
  218.2 1.0 fusion.2
  219.2 1.0 copy.36
  (1 shorter events, 0.0 us)
Async XLA Ops:
  6.2 15.7 %copy-start.6 = (s32[1,1,4,3]{2,1,3,0:T(1,128)S(1)}, s32[1,1,4,3]{2,1,3,0:T(1,128)}, u32[]{:S(2)}) copy-start(s32[1,1,4,3]{2,1,3,0:T(1,128)} %param.13) | copy-start | bytes 148
  6.2 15.8 %copy-start.7 = (s32[1,1,4,2]{2,3,1,0:T(2,128)S(1)}, s32[1,1,4,2]{2,3,1,0:T(2,128)}, u32[]{:S(2)}) copy-start(s32[1,1,4,2]{2,3,1,0:T(2,128)} %param.12) | copy-start | bytes 100
  6.2 69.6 %all-to-all-start = ((bf16[256,4,2,2,256]{4,3,2,1,0:T(2,128)(2,1)}), bf16[256,4,2,2,256]{4,3,2,1,0:T(2,128)(2,1)S(1)}, u32[]{:S(2)}, u32[]{:S(2)}) async-start(bf16[256,4,2,2,256]{4,3,2,1,0:T(2,128)(2,1)} %bitcast.34), calls=%async_computation | async-start | bytes 4194304 | tf_op jit(solution)/shard_map/all_to_all | solution.py:203
  80.0 2.9 %copy-start.1 = (f32[16,64,256]{2,1,0:T(8,128)S(1)}, f32[16,64,256]{2,1,0:T(8,128)}, u32[]{:S(2)}) copy-start(f32[16,64,256]{2,1,0:T(8,128)} %constant.14.clone.green) | copy-start | bytes 3145732
  80.0 2.9 %copy-start.2 = (bf16[768,256]{1,0:T(8,128)(2,1)S(1)}, bf16[768,256]{1,0:T(8,128)(2,1)}, u32[]{:S(2)}) copy-start(bf16[768,256]{1,0:T(8,128)(2,1)} %constant.13.clone.bd) | copy-start | bytes 1179652
  82.9 0.8 copy-start.3
  83.6 0.8 copy-start.4
  84.4 0.8 copy-start.5
  135.3 1.3 copy-start

commit v2 on v1

--- a/solution.py
+++ b/solution.py
@@ -31,7 +31,8 @@
         hi, lo = parts(a)
         return np.concatenate([hi, hi, lo], axis=1)
 
-    cx = left(cas)
+    cx = left(cas[:, perm])
+    ux = left(cas[perm, :])
     cf = left(cas[:, perm])
     ci = left(cas[perm, :])
     hi, lo = parts(np.kron(np.eye(4), cas))
@@ -39,7 +40,7 @@
     e = 2.0 - 2.0 * np.cos(2.0 * math.pi * m / N)
     green = 1.0 / ((screening + e[:, None, None] + e[None, :, None] + e[None, None, :]) * float(N**3))
     g = green.reshape(CH, 4, N, N).transpose(0, 2, 1, 3).reshape(CH, N, W).astype(np.float32)
-    return cx, cf, ci, bd, g
+    return cx, ux, bd, g
 
 
 def split(v):
@@ -62,7 +63,7 @@
     return mm(jnp.concatenate([hi, lo, hi], axis=1), bd)
 
 
-def pair_kernel(slots, offs, count, box, cx, cf, ci, bd, green, out, pad, sh, U, wh, wl, col):
+def pair_kernel(slots, offs, count, land, cx, ux, bd, green, out, box, pad, sh, U, F, wh, wl, col):
     GR = 4
     low = lax.broadcasted_iota(jnp.int32, (32, 128), 1) < 64
     zpad = jnp.zeros((4, N, W), bf16)
@@ -70,6 +71,24 @@
         r[0:4] = zpad
         r[20:24] = zpad
     col[...] = jnp.zeros(col.shape, f32)
+    place = lax.axis_index("pair")
+
+    def arrange(s, c):
+        def widen(g, c2):
+            for k in range(8):
+                F[pl.ds(pl.multiple_of(g * PITCH, 8) + 8 * k, 8), :] = land[k, g, s].astype(f32)
+            return c2
+
+        lax.fori_loop(0, 32, widen, 0)
+        for k in range(8):
+            j = (place + k) % 8 * 2
+            for jj in range(2):
+                for half in range(2):
+                    two = [F[pl.ds(8 * k + 4 * jj + 2 * half + xx, 32, stride=PITCH), :] for xx in range(2)]
+                    box[s, j + jj, :, half * 128:(half + 1) * 128] = jnp.concatenate(two, axis=0).astype(bf16)
+        return c
+
+    lax.fori_loop(0, 4, arrange, 0)
 
     def pair(k, carry):
         a = slots[k, 0]
@@ -95,6 +114,8 @@
         bwd = jnp.concatenate([b0, b0, b1, b1], axis=0)
         xr = lax.broadcasted_iota(jnp.int32, (N, N), 0)
         xc = lax.broadcasted_iota(jnp.int32, (N, N), 1)
+        xr = xr % 32 * 2 + xr // 32
+        xc = xc % 32 * 2 + xc // 32
         sx = mask(xc == xr + dx)
         sxt = mask(xr == xc + dx)
 
@@ -127,8 +148,8 @@
                 tops.append(jnp.where(low, l1, pltpu.roll(l2, 64, 1)))
                 bots.append(jnp.where(low, pltpu.roll(l1, 64, 1), l2))
             v = jnp.concatenate([jnp.concatenate(tops, axis=1), jnp.concatenate(bots, axis=1)], axis=0)
-            s = left_mul(cf[...], v) * green[g]
-            p = left_mul(ci[...], s)
+            s = left_mul(cx[...], v) * green[g]
+            p = left_mul(ux[...], s)
             for h in range(2):
                 x0 = p[:32, h * 128:(h + 1) * 128]
                 x1 = p[32:, h * 128:(h + 1) * 128]
@@ -144,7 +165,7 @@
             for i in range(GR):
                 v = jnp.concatenate(
                     [U[pl.ds(pl.multiple_of((2 * (lo_ + i) + h) * PITCH, 8), N), :] for h in range(2)], axis=1)
-                outs.append(left_mul(cx[...], v))
+                outs.append(left_mul(ux[...], v))
             pot = right_mul(jnp.concatenate(outs, axis=0), bd[...]).reshape(GR, N, W)
             for i in range(GR):
                 j = lo_ + i
@@ -168,21 +189,40 @@
         return carry
 
     lax.fori_loop(0, count[0], pair, 0)
-    out[...] = col[...].astype(bf16)
-
-
-def worker_fields(box, slots, offs, count):
-    cx, cf, ci, bd, g = (jnp.asarray(t) for t in tables())
+
+    def deliver(s, c):
+        for k in range(8):
+            for jj in range(2):
+                for half in range(2):
+                    for xx in range(2):
+                        F[pl.ds(8 * k + 4 * jj + 2 * half + xx, 32, stride=PITCH), :] = (
+                            col[s, 2 * k + jj, xx * 32:(xx + 1) * 32, half * 128:(half + 1) * 128])
+
+        def narrow(g, c2):
+            for k in range(8):
+                out[g, k, s] = F[pl.ds(pl.multiple_of(g * PITCH, 8) + 8 * k, 8), :].astype(bf16)
+            return c2
+
+        lax.fori_loop(0, 32, narrow, 0)
+        return c
+
+    lax.fori_loop(0, 4, deliver, 0)
+
+
+def worker_fields(land, slots, offs, count):
+    cx, ux, bd, g = (jnp.asarray(t) for t in tables())
     smem = pl.BlockSpec(memory_space=pltpu.SMEM)
     vmem = pl.BlockSpec(memory_space=pltpu.VMEM)
     return pl.pallas_call(
         pair_kernel,
-        out_shape=jax.ShapeDtypeStruct((4, CH, N, W), bf16),
-        in_specs=[smem] * 3 + [vmem] * 6,
+        out_shape=jax.ShapeDtypeStruct((32, 8, 4, 8, 128), bf16),
+        in_specs=[smem] * 3 + [vmem] * 5,
         out_specs=vmem,
         scratch_shapes=[
+            pltpu.VMEM((4, CH, N, W), bf16),
             pltpu.VMEM((24, N, W), bf16),
             pltpu.VMEM((CH, N, W), bf16),
+            pltpu.VMEM((32 * PITCH, 128), f32),
             pltpu.VMEM((32 * PITCH, 128), f32),
             pltpu.VMEM((24, N, W), bf16),
             pltpu.VMEM((24, N, W), bf16),
@@ -190,23 +230,129 @@
         ],
         compiler_params=pltpu.CompilerParams(vmem_limit_bytes=40 << 20),
         name="pairs",
-    )(slots, offs, count, box, cx, cf, ci, bd, g)
+    )(slots, offs, count, land, cx, ux, bd, g)
+
+
+MESH = pl.DeviceIdType.MESH
+SUBS = 4
+
+
+def gather_kernel(gy, gx, orb, lists, land, *rest):
+    blocks = rest[:7]
+    send, zsend, zrecv, ssem, rsem = rest[7:]
+    G = gy * gx * 2
+    me = lax.axis_index("grid")
+    p = lax.axis_index("pair")
+    my_y, my_x, my_c = me // (2 * gx), (me // 2) % gx, me % 2
+    right, left = (p + 1) % 8, (p + 7) % 8
+    held = (orb,) + tuple(blocks)
+    rows = orb.shape[0] // SUBS
+
+    def peer(i):
+        y = (my_y + i // (2 * gx)) % gy
+        x = (my_x + (i // 2) % gx) % gx
+        c = (my_c + i) % 2
+        return (y * gx + x) * 2 + c
+
+    barrier = pltpu.get_barrier_semaphore()
+    pl.semaphore_signal(barrier, inc=1, device_id=(me, right), device_id_type=MESH)
+    pl.semaphore_signal(barrier, inc=1, device_id=(me, left), device_id_type=MESH)
+
+    def greet(i, c):
+        pl.semaphore_signal(barrier, inc=1, device_id=(peer(i), p), device_id_type=MESH)
+        return c
+
+    lax.fori_loop(1, G, greet, 0)
+    pl.semaphore_wait(barrier, G + 1)
+
+    def hop(d, h, sub):
+        src, dst = (h - 1, h) if d == 0 else ((9 - h) % 8, 8 - h)
+        part = pl.ds(sub * rows, rows)
+        return pltpu.make_async_remote_copy(
+            src_ref=held[src].at[part], dst_ref=held[dst].at[part],
+            send_sem=zsend.at[d, h - 1, sub], recv_sem=zrecv.at[d, h - 1, sub],
+            device_id=(me, left if d == 0 else right), device_id_type=MESH)
+
+    def used(d, h, sub):
+        return h < 4 or (h == 4 and (sub < SUBS // 2) == (d == 0))
+
+    def spread(k):
+        block = held[k]
+
+        def pick(i, c):
+            base = (peer(i) * 8 + p) * 4
+            for s in range(4):
+                send[k, i, s] = block[lists[base + s]]
+            return c
+
+        lax.fori_loop(0, G, pick, 0)
+
+        def push(i, c):
+            pltpu.make_async_remote_copy(
+                src_ref=send.at[k, i], dst_ref=land.at[k, me], send_sem=ssem.at[k], recv_sem=rsem.at[k],
+                device_id=(peer(i), p), device_id_type=MESH).start()
+            return c
+
+        pltpu.make_async_copy(send.at[k, 0], land.at[k, me], rsem.at[k]).start()
+        lax.fori_loop(1, G, push, 0)
+
+    for sub in range(SUBS):
+        for d in range(2):
+            hop(d, 1, sub).start()
+    spread(0)
+    for h in range(1, 5):
+        for sub in range(SUBS):
+            for d in range(2):
+                if used(d, h, sub):
+                    hop(d, h, sub).wait_recv()
+                    if used(d, h + 1, sub):
+                        hop(d, h + 1, sub).start()
+        spread(h)
+        if h < 4:
+            spread(8 - h)
+    for h in range(1, 5):
+        for sub in range(SUBS):
+            for d in range(2):
+                if used(d, h, sub):
+                    hop(d, h, sub).wait_send()
+    for k in range(8):
+        pltpu.make_async_remote_copy(
+            src_ref=send.at[k, pl.ds(1, G - 1)], dst_ref=land.at[k, pl.ds(1, G - 1)],
+            send_sem=ssem.at[k], recv_sem=rsem.at[k], device_id=(me, right), device_id_type=MESH).wait_send()
+        pltpu.make_async_copy(land.at[k], land.at[k], rsem.at[k]).wait()
+
+
+def gather_boxes(orb, lists, gy, gx):
+    G = gy * gx * 2
+    norb = orb.shape[0]
+    vmem = pl.BlockSpec(memory_space=pltpu.VMEM)
+    return pl.pallas_call(
+        lambda *refs: gather_kernel(gy, gx, *refs),
+        out_shape=jax.ShapeDtypeStruct((8, G, 4, 8, 128), bf16),
+        in_specs=[vmem, pl.BlockSpec(memory_space=pltpu.SMEM)],
+        out_specs=vmem,
+        scratch_shapes=[pltpu.VMEM((norb, 8, 128), bf16)] * 7 + [
+            pltpu.VMEM((8, G, 4, 8, 128), bf16),
+            pltpu.SemaphoreType.DMA((2, 4, SUBS)),
+            pltpu.SemaphoreType.DMA((2, 4, SUBS)),
+            pltpu.SemaphoreType.DMA((8,)),
+            pltpu.SemaphoreType.DMA((8,)),
+        ],
+        compiler_params=pltpu.CompilerParams(collective_id=0, has_side_effects=True, vmem_limit_bytes=24 << 20),
+        name="gather_boxes",
+    )(orb, lists)
 
 
 def shards(orbitals, box_list, pair_slots, offsets, pair_count):
     planes, orbital_total, row_cells = orbitals.shape
     lists = box_list.reshape(-1)
+    orb = orbitals.reshape(planes, orbital_total, 4, 128).transpose(1, 2, 0, 3).reshape(orbital_total, 8, 128)
+    land = gather_boxes(orb, lists, 4, 4)
+    back = worker_fields(land, pair_slots[0, 0], offsets[0, 0], pair_count[0])
+    landed = lax.all_to_all(back.reshape(256, 4, 8, 128), ("grid", "pair"), split_axis=0, concat_axis=0, tiled=True)
     hot = (lists[:, None] == jnp.arange(orbital_total, dtype=jnp.int32)[None, :]).astype(bf16)
-    local = orbitals.reshape(planes, orbital_total, 2, W)
-    picked = jnp.einsum("ro,xojc->rjxc", hot, local, preferred_element_type=f32).astype(bf16)
-    picked = picked.reshape(256, 4, 2, planes, W)
-    arrived = lax.all_to_all(picked, ("grid", "pair"), split_axis=0, concat_axis=0, tiled=True)
-    box = arrived.reshape(32, 8, 4, 2, planes, W).transpose(2, 1, 3, 0, 4, 5).reshape(4, CH, N, W)
-    fields = worker_fields(box, pair_slots[0, 0], offsets[0, 0], pair_count[0])
-    back = fields.reshape(4, 8, 2, 32, planes, W).transpose(3, 1, 0, 2, 4, 5).reshape(256, 4, 2, planes, W)
-    landed = lax.all_to_all(back, ("grid", "pair"), split_axis=0, concat_axis=0, tiled=True)
-    landed = landed.reshape(1024, 2, planes, W)
-    summed = jnp.einsum("ro,rjxc->xojc", hot, landed, preferred_element_type=f32)
+    landed = landed.reshape(1024, 4, planes, 128)
+    summed = jnp.einsum("ro,rqxc->xoqc", hot, landed, preferred_element_type=f32)
     return summed.reshape(planes, orbital_total, row_cells)
 
 

time: 221 us -> 182 us (0.82)
  waiting for transfers between devices: 53 us -> 0 us
  Pallas kernels: 50.2 us -> 97.7 us
  local copies, waits for them, and re-layouts: 22.6 us -> 4.97 us
  starting transfers between devices: 15.6 us -> 0 us
    all_to_all x1 -> x0, waiting for transfers between devices: 53 us -> none  [shards(): lax.all_to_all(picked, ('grid', 'pair'), split_axis=0, concat_axis=0, til...]
    pallas_call x1 -> x2, Pallas kernels: 50.2 us -> 97.7 us  [the longest x1 53.3 us: worker_fields(): pl.pallas_call(pair_kernel, out_shape=jax.ShapeDtypeStruct((32, 8, 4, 8,...]
    all_to_all x1 -> x0, starting transfers between devices: 15.6 us -> none  [shards(): lax.all_to_all(picked, ('grid', 'pair'), split_axis=0, concat_axis=0, til...]
    reshape x5 -> x3, local copies, waits for them, and re-layouts: 12.5 us -> 1.54 us  [the longest x2 1.42 us: shards(): orbitals.reshape(planes, orbital_total, 4, 128).transpose(1, 2, 0, 3)]
    transpose x2 -> x1, local copies, waits for them, and re-layouts: 3.56 us -> 0.04 us  [shards(): jnp.einsum('ro,rqxc->xoqc', hot, landed, preferred_element_type=f32)]
    unnamed x18 -> x10, local copies, waits for them, and re-layouts: 4.56 us -> 1.63 us
  transfers between devices with their start and end apart: 1 -> 0, of which waited for: 1 -> 0; matrix products, arithmetic and copies ran while one was open for 0% -> 0% of each run, Pallas kernels for 0% -> 0%
where the time goes in v2:
time: 182 us
  Pallas kernels  97.7 us (54%)
  blocking collectives  77.4 us (43%)
  local copies, waits for them, and re-layouts  4.97 us (3%)
    all_to_all x1, blocking collectives, shards(): lax.all_to_all(back.reshape(256, 4, 8, 128), ('grid', 'pair'), split_axis...  77.4 us
    pallas_call x1, Pallas kernels, worker_fields(): pl.pallas_call(pair_kernel, out_shape=jax.ShapeDtypeStruct((32, 8, 4, 8,...  53.3 us
    pallas_call x1, Pallas kernels, gather_boxes(): pl.pallas_call(lambda *refs: gather_kernel(gy, gx, *refs), out_shape=jax....  44.4 us

profile of v2, /device:TPU:1, one launch (start us, length us, event | category | flops | bytes accessed | tf_op | source)
XLA Modules:
  0.0 181.8 jit_solution(569440798904959517)
XLA Ops:
  0.0 0.0 copy-start
  0.0 0.0 copy-start.1
  0.0 0.0 copy-start.2
  0.0 0.0 copy-start.3
  0.8 0.8 copy.17.slots
  1.5 0.8 copy.14
  2.3 0.9 copy.16
  3.2 0.1 reshape.21.refs_1_
  3.3 1.0 reshape.19
  4.3 0.4 copy.15
  4.7 44.4 %gather_boxes.1.land = bf16[8,32,4,8,128]{4,3,2,1,0:T(8,128)(2,1)S(1)} custom-call(bf16[128,8,128]{2,1,0:T(8,128)(2,1)S(1)} %bitcast.18, s32[1024]{0:T(1024)S(1)} %reshape.21.refs_1_), custom_call_target="tpu_custom_call" | custom-call | tf_op jit(solution)/shard_map/gather_boxes/pallas_call | solution.py:329
  49.1 0.0 copy-done
  49.1 0.0 copy-done.1
  49.1 0.0 copy-done.2
  49.1 0.0 copy-done.3
  49.1 53.3 %pairs.1 = bf16[32,8,4,8,128]{4,3,2,1,0:T(8,128)(2,1)S(1)} custom-call(s32[4,2]{1,0:T(4,128)S(1)} %copy.17.slots, s32[4,3]{1,0:T(4,128)S(1)} %bitcast.19, s32[1]{0:T(128)} %bitcast.16.count, bf16[8,32,4,8,128]{4,3,2,1,0:T(8,128)(2,1)S(1)} %gather_boxes.1.land, bf16[64,192]{1,0:T(8,128)(2,1)S(1)} %copy-done.3, bf16[64,192]{1,0:T(8,128)(2,1)S(1)} %copy-done.2, ...), custom_call_target="tpu_custom_call" | custom-call | tf_op jit(solution)/shard_map/pairs/pallas_call | solution.py:216
  102.4 77.4 %all_to_all.5 = bf16[256,4,8,128]{3,2,1,0:T(8,128)(2,1)S(1)} all-to-all(bf16[256,4,8,128]{3,2,1,0:T(8,128)(2,1)S(1)} %bitcast.17), channel_id=1, replica_groups=mesh['grid'=32,'pair'=8] {'grid','pair'}, dimensions={0} | all-to-all | bytes 4194304 | tf_op jit(solution)/shard_map/all_to_all | solution.py:352
  179.8 1.0 fusion.2
  180.8 1.0 copy.20
  (1 shorter events, 0.0 us)
Async XLA Ops:
  0.0 49.1 %copy-start = (f32[16,64,256]{2,1,0:T(8,128)S(1)}, f32[16,64,256]{2,1,0:T(8,128)}, u32[]{:S(2)}) copy-start(f32[16,64,256]{2,1,0:T(8,128)} %constant.11.clone.green) | copy-start | bytes 3145732
  0.0 49.1 %copy-start.1 = (bf16[768,256]{1,0:T(8,128)(2,1)S(1)}, bf16[768,256]{1,0:T(8,128)(2,1)}, u32[]{:S(2)}) copy-start(bf16[768,256]{1,0:T(8,128)(2,1)} %constant.10.clone.bd) | copy-start | bytes 1179652
  0.0 49.1 %copy-start.2 = (bf16[64,192]{1,0:T(8,128)(2,1)S(1)}, bf16[64,192]{1,0:T(8,128)(2,1)}, u32[]{:S(2)}) copy-start(bf16[64,192]{1,0:T(8,128)(2,1)} %constant.9.clone.ux) | copy-start | bytes 73732
  0.0 49.1 %copy-start.3 = (bf16[64,192]{1,0:T(8,128)(2,1)S(1)}, bf16[64,192]{1,0:T(8,128)(2,1)}, u32[]{:S(2)}) copy-start(bf16[64,192]{1,0:T(8,128)(2,1)} %constant.8.clone.cx) | copy-start | bytes 73732

commit v3 on v2

--- a/solution.py
+++ b/solution.py
@@ -63,14 +63,15 @@
     return mm(jnp.concatenate([hi, lo, hi], axis=1), bd)
 
 
-def pair_kernel(slots, offs, count, land, cx, ux, bd, green, out, box, pad, sh, U, F, wh, wl, col):
-    GR = 4
+def pair_kernel(slots, offs, count, land, cx, ux, bd, green, out, box, pad, X, U, F, wh, wl, col):
+    GR = 16
     low = lax.broadcasted_iota(jnp.int32, (32, 128), 1) < 64
     zpad = jnp.zeros((4, N, W), bf16)
     for r in (pad, wh, wl):
         r[0:4] = zpad
         r[20:24] = zpad
     col[...] = jnp.zeros(col.shape, f32)
+    X[...] = jnp.zeros(X.shape, f32)
     place = lax.axis_index("pair")
 
     def arrange(s, c):
@@ -112,25 +113,33 @@
         b0 = mask(okr & (cols == rows + r))
         b1 = mask(okr & (cols == rows + r - 256))
         bwd = jnp.concatenate([b0, b0, b1, b1], axis=0)
-        xr = lax.broadcasted_iota(jnp.int32, (N, N), 0)
-        xc = lax.broadcasted_iota(jnp.int32, (N, N), 1)
-        xr = xr % 32 * 2 + xr // 32
-        xc = xc % 32 * 2 + xc // 32
-        sx = mask(xc == xr + dx)
-        sxt = mask(xr == xc + dx)
-
         pad[4:20] = box[b]
+
+        def put(j, v):
+            for h in range(2):
+                for e in range(2):
+                    X[j, h, e * 48 + 8:e * 48 + 40, :] = v[e * 32:(e + 1) * 32, h * 128:(h + 1) * 128]
+
+        def moved(j, step):
+            halves = []
+            for h in range(2):
+                both = []
+                for e in range(2):
+                    n = step + 16 + e
+                    both.append(X[j, h, pl.ds(n % 2 * 48 + n // 2, 32), :])
+                halves.append(jnp.concatenate(both, axis=0))
+            return jnp.concatenate(halves, axis=1)
 
         def forward(g, c):
             lo_ = g * GR
             src0 = pad[pl.ds(lo_ + 4 + q, GR)].reshape(GR * N, W)
             src1 = pad[pl.ds(lo_ + 5 + q, GR)].reshape(GR * N, W)
-            yz = mm(jnp.concatenate([src0, src1], axis=1), fwd).astype(bf16).reshape(GR, N, W)
+            yz = mm(jnp.concatenate([src0, src1], axis=1), fwd).reshape(GR, N, W)
+            for i in range(GR):
+                put(lo_ + i, yz[i])
             outs = []
             for i in range(GR):
-                s = mm(sx, yz[i])
-                sh[lo_ + i] = s.astype(bf16)
-                dens = box[a, lo_ + i].astype(f32) * s
+                dens = box[a, lo_ + i].astype(f32) * moved(lo_ + i, dx)
                 outs.append(left_mul(cx[...], dens))
             spec = right_mul(jnp.concatenate(outs, axis=0), bd[...])
             for i in range(GR):
@@ -157,7 +166,7 @@
                 U[pl.ds(g * 4 + 2 * h + 1, 32, stride=PITCH), :] = jnp.where(low, pltpu.roll(x0, 64, 1), x1)
             return c
 
-        lax.fori_loop(0, CH, middle, 0)
+        lax.fori_loop(0, CH, middle, 0, unroll=8)
 
         def inverse(g, c):
             lo_ = g * GR
@@ -169,10 +178,9 @@
             pot = right_mul(jnp.concatenate(outs, axis=0), bd[...]).reshape(GR, N, W)
             for i in range(GR):
                 j = lo_ + i
-                col[a, j] = col[a, j] - pot[i] * sh[j].astype(f32)
-                hi, lo = split(-(pot[i] * box[a, j].astype(f32)))
-                wh[j + 4] = mm(sxt, hi).astype(bf16)
-                wl[j + 4] = mm(sxt, lo).astype(bf16)
+                col[a, j] = col[a, j] - pot[i] * moved(j, dx)
+                put(j, -(pot[i] * box[a, j].astype(f32)))
+                wh[j + 4], wl[j + 4] = split(moved(j, -dx))
             return c
 
         lax.fori_loop(0, CH // GR, inverse, 0)
@@ -221,7 +229,7 @@
         scratch_shapes=[
             pltpu.VMEM((4, CH, N, W), bf16),
             pltpu.VMEM((24, N, W), bf16),
-            pltpu.VMEM((CH, N, W), bf16),
+            pltpu.VMEM((CH, 2, 96, 128), f32),
             pltpu.VMEM((32 * PITCH, 128), f32),
             pltpu.VMEM((32 * PITCH, 128), f32),
             pltpu.VMEM((24, N, W), bf16),
@@ -263,7 +271,6 @@
         return c
 
     lax.fori_loop(1, G, greet, 0)
-    pl.semaphore_wait(barrier, G + 1)
 
     def hop(d, h, sub):
         src, dst = (h - 1, h) if d == 0 else ((9 - h) % 8, 8 - h)
@@ -276,30 +283,35 @@
     def used(d, h, sub):
         return h < 4 or (h == 4 and (sub < SUBS // 2) == (d == 0))
 
-    def spread(k):
+    def pick(k):
         block = held[k]
 
-        def pick(i, c):
-            base = (peer(i) * 8 + p) * 4
-            for s in range(4):
-                send[k, i, s] = block[lists[base + s]]
-            return c
-
-        lax.fori_loop(0, G, pick, 0)
-
-        def push(i, c):
+        def some(t, c):
+            for i in range(4):
+                g = t * 4 + i
+                for s in range(4):
+                    send[k, g, s] = block[lists[(g * 8 + p) * 4 + s]]
+            return c
+
+        lax.fori_loop(0, G // 4, some, 0)
+
+    def push(k):
+        def one(i, c):
+            g = peer(i)
             pltpu.make_async_remote_copy(
-                src_ref=send.at[k, i], dst_ref=land.at[k, me], send_sem=ssem.at[k], recv_sem=rsem.at[k],
-                device_id=(peer(i), p), device_id_type=MESH).start()
-            return c
-
-        pltpu.make_async_copy(send.at[k, 0], land.at[k, me], rsem.at[k]).start()
-        lax.fori_loop(1, G, push, 0)
-
+                src_ref=send.at[k, g], dst_ref=land.at[k, me], send_sem=ssem.at[k], recv_sem=rsem.at[k],
+                device_id=(g, p), device_id_type=MESH).start()
+            return c
+
+        pltpu.make_async_copy(send.at[k, me], land.at[k, me], rsem.at[k]).start()
+        lax.fori_loop(1, G, one, 0)
+
+    pick(0)
+    pl.semaphore_wait(barrier, G + 1)
     for sub in range(SUBS):
         for d in range(2):
             hop(d, 1, sub).start()
-    spread(0)
+    push(0)
     for h in range(1, 5):
         for sub in range(SUBS):
             for d in range(2):
@@ -307,9 +319,9 @@
                     hop(d, h, sub).wait_recv()
                     if used(d, h + 1, sub):
                         hop(d, h + 1, sub).start()
-        spread(h)
-        if h < 4:
-            spread(8 - h)
+        for k in (h, 8 - h) if h < 4 else (h,):
+            pick(k)
+            push(k)
     for h in range(1, 5):
         for sub in range(SUBS):
             for d in range(2):

time: 182 us -> 139 us (0.76)
  Pallas kernels: 97.7 us -> 65 us
  blocking collectives: 77.4 us -> 66.6 us
    pallas_call x1, Pallas kernels: 53.3 us -> 21.5 us  [worker_fields(): pl.pallas_call(pair_kernel, out_shape=jax.ShapeDtypeStruct((32, 8, 4, 8,...]
    all_to_all x1, blocking collectives: 77.4 us -> 66.6 us  [shards(): lax.all_to_all(back.reshape(256, 4, 8, 128), ('grid', 'pair'), split_axis...]
where the time goes in v3:
time: 139 us; the launch traced here: 138 us
  blocking collectives  66.6 us (48%)
  Pallas kernels  65 us (47%)
  local copies, waits for them, and re-layouts  4.97 us (4%)
    all_to_all x1, blocking collectives, shards(): lax.all_to_all(back.reshape(256, 4, 8, 128), ('grid', 'pair'), split_axis...  66.6 us
    pallas_call x1, Pallas kernels, gather_boxes(): pl.pallas_call(lambda *refs: gather_kernel(gy, gx, *refs), out_shape=jax....  43.5 us
    pallas_call x1, Pallas kernels, worker_fields(): pl.pallas_call(pair_kernel, out_shape=jax.ShapeDtypeStruct((32, 8, 4, 8,...  21.5 us

profile of v3, /device:TPU:1, one launch (start us, length us, event | category | flops | bytes accessed | tf_op | source)
XLA Modules:
  0.0 138.4 jit_solution(7183822425741227413)
XLA Ops:
  0.0 0.0 copy-start
  0.0 0.0 copy-start.1
  0.0 0.0 copy-start.2
  0.0 0.0 copy-start.3
  0.8 0.8 copy.17.slots
  1.5 0.8 copy.14
  2.3 0.9 copy.16
  3.2 0.1 reshape.21.refs_1_
  3.3 1.0 reshape.19
  4.3 0.4 copy.15
  4.7 43.5 %gather_boxes.1.land = bf16[8,32,4,8,128]{4,3,2,1,0:T(8,128)(2,1)S(1)} custom-call(bf16[128,8,128]{2,1,0:T(8,128)(2,1)S(1)} %bitcast.18, s32[1024]{0:T(1024)S(1)} %reshape.21.refs_1_), custom_call_target="tpu_custom_call" | custom-call | tf_op jit(solution)/shard_map/gather_boxes/pallas_call | solution.py:341
  48.2 0.0 copy-done
  48.2 0.0 copy-done.1
  48.2 0.0 copy-done.2
  48.3 0.0 copy-done.3
  48.3 21.5 %pairs.1 = bf16[32,8,4,8,128]{4,3,2,1,0:T(8,128)(2,1)S(1)} custom-call(s32[4,2]{1,0:T(4,128)S(1)} %copy.17.slots, s32[4,3]{1,0:T(4,128)S(1)} %bitcast.19, s32[1]{0:T(128)} %bitcast.16.count, bf16[8,32,4,8,128]{4,3,2,1,0:T(8,128)(2,1)S(1)} %gather_boxes.1.land, bf16[64,192]{1,0:T(8,128)(2,1)S(1)} %copy-done.3, bf16[64,192]{1,0:T(8,128)(2,1)S(1)} %copy-done.2, ...), custom_call_target="tpu_custom_call" | custom-call | tf_op jit(solution)/shard_map/pairs/pallas_call | solution.py:224
  69.8 66.6 %all_to_all.5 = bf16[256,4,8,128]{3,2,1,0:T(8,128)(2,1)S(1)} all-to-all(bf16[256,4,8,128]{3,2,1,0:T(8,128)(2,1)S(1)} %bitcast.17), channel_id=1, replica_groups=mesh['grid'=32,'pair'=8] {'grid','pair'}, dimensions={0} | all-to-all | bytes 4194304 | tf_op jit(solution)/shard_map/all_to_all | solution.py:364
  136.4 1.0 fusion.2
  137.4 1.0 copy.20
  (1 shorter events, 0.0 us)
Async XLA Ops:
  0.0 48.2 %copy-start = (f32[16,64,256]{2,1,0:T(8,128)S(1)}, f32[16,64,256]{2,1,0:T(8,128)}, u32[]{:S(2)}) copy-start(f32[16,64,256]{2,1,0:T(8,128)} %constant.11.clone.green) | copy-start | bytes 3145732
  0.0 48.2 %copy-start.1 = (bf16[768,256]{1,0:T(8,128)(2,1)S(1)}, bf16[768,256]{1,0:T(8,128)(2,1)}, u32[]{:S(2)}) copy-start(bf16[768,256]{1,0:T(8,128)(2,1)} %constant.10.clone.bd) | copy-start | bytes 1179652
  0.0 48.2 %copy-start.2 = (bf16[64,192]{1,0:T(8,128)(2,1)S(1)}, bf16[64,192]{1,0:T(8,128)(2,1)}, u32[]{:S(2)}) copy-start(bf16[64,192]{1,0:T(8,128)(2,1)} %constant.9.clone.ux) | copy-start | bytes 73732
  0.0 48.3 %copy-start.3 = (bf16[64,192]{1,0:T(8,128)(2,1)S(1)}, bf16[64,192]{1,0:T(8,128)(2,1)}, u32[]{:S(2)}) copy-start(bf16[64,192]{1,0:T(8,128)(2,1)} %constant.8.clone.cx) | copy-start | bytes 73732

commit v4 on v3

--- a/solution.py
+++ b/solution.py
@@ -12,6 +12,7 @@
 CH = 16
 W = 256
 PITCH = 72
+PITCH2 = 24
 f32, bf16 = jnp.float32, jnp.bfloat16
 
 
@@ -75,12 +76,14 @@
     place = lax.axis_index("pair")
 
     def arrange(s, c):
-        def widen(g, c2):
-            for k in range(8):
-                F[pl.ds(pl.multiple_of(g * PITCH, 8) + 8 * k, 8), :] = land[k, g, s].astype(f32)
+        def widen(t, c2):
+            for i in range(4):
+                g = t * 4 + i
+                for k in range(8):
+                    F[pl.ds(pl.multiple_of(g * PITCH, 8) + 8 * k, 8), :] = land[k, g, s].astype(f32)
             return c2
 
-        lax.fori_loop(0, 32, widen, 0)
+        lax.fori_loop(0, 8, widen, 0)
         for k in range(8):
             j = (place + k) % 8 * 2
             for jj in range(2):
@@ -92,9 +95,9 @@
     lax.fori_loop(0, 4, arrange, 0)
 
     def pair(k, carry):
-        a = slots[k, 0]
-        b = slots[k, 1]
-        dx, dy, dz = offs[k, 0], offs[k, 1], offs[k, 2]
+        a = slots[0, k]
+        b = slots[1, k]
+        dx, dy, dz = offs[0, 0, k], offs[1, 0, k], offs[2, 0, k]
         t = dy * 64 + dz
         q = (t + 1024) // 256 - 4
         r = t - 256 * q
@@ -196,25 +199,28 @@
         lax.fori_loop(0, CH // GR, back, 0)
         return carry
 
-    lax.fori_loop(0, count[0], pair, 0)
-
-    def deliver(s, c):
-        for k in range(8):
+    lax.fori_loop(0, count[0, 0], pair, 0)
+
+    def deliver(k, c):
+        j = (place + k) % 8 * 2
+        for s in range(4):
             for jj in range(2):
                 for half in range(2):
                     for xx in range(2):
-                        F[pl.ds(8 * k + 4 * jj + 2 * half + xx, 32, stride=PITCH), :] = (
-                            col[s, 2 * k + jj, xx * 32:(xx + 1) * 32, half * 128:(half + 1) * 128])
-
-        def narrow(g, c2):
-            for k in range(8):
-                out[g, k, s] = F[pl.ds(pl.multiple_of(g * PITCH, 8) + 8 * k, 8), :].astype(bf16)
+                        F[pl.ds(32 * PITCH2 * half + 4 * s + 2 * jj + xx, 32, stride=PITCH2), :] = (
+                            col[s, j + jj, xx * 32:(xx + 1) * 32, half * 128:(half + 1) * 128])
+
+        def narrow(t, c2):
+            for i in range(4):
+                g = t * 4 + i
+                for half in range(2):
+                    out[k, g, half] = F[pl.ds(pl.multiple_of((half * 32 + g) * PITCH2, 8), 16), :].astype(bf16)
             return c2
 
-        lax.fori_loop(0, 32, narrow, 0)
+        lax.fori_loop(0, 8, narrow, 0)
         return c
 
-    lax.fori_loop(0, 4, deliver, 0)
+    lax.fori_loop(0, 8, deliver, 0)
 
 
 def worker_fields(land, slots, offs, count):
@@ -223,7 +229,7 @@
     vmem = pl.BlockSpec(memory_space=pltpu.VMEM)
     return pl.pallas_call(
         pair_kernel,
-        out_shape=jax.ShapeDtypeStruct((32, 8, 4, 8, 128), bf16),
+        out_shape=jax.ShapeDtypeStruct((8, 32, 2, 16, 128), bf16),
         in_specs=[smem] * 3 + [vmem] * 5,
         out_specs=vmem,
         scratch_shapes=[
@@ -236,7 +242,7 @@
             pltpu.VMEM((24, N, W), bf16),
             pltpu.VMEM((4, CH, N, W), f32),
         ],
-        compiler_params=pltpu.CompilerParams(vmem_limit_bytes=40 << 20),
+        compiler_params=pltpu.CompilerParams(vmem_limit_bytes=28 << 20),
         name="pairs",
     )(slots, offs, count, land, cx, ux, bd, g)
 
@@ -246,15 +252,18 @@
 
 
 def gather_kernel(gy, gx, orb, lists, land, *rest):
-    blocks = rest[:7]
-    send, zsend, zrecv, ssem, rsem = rest[7:]
+    blocks = rest[:8]
+    wide, send, zsend, zrecv, ssem, rsem = rest[8:]
     G = gy * gx * 2
     me = lax.axis_index("grid")
     p = lax.axis_index("pair")
     my_y, my_x, my_c = me // (2 * gx), (me // 2) % gx, me % 2
     right, left = (p + 1) % 8, (p + 7) % 8
-    held = (orb,) + tuple(blocks)
-    rows = orb.shape[0] // SUBS
+    held = blocks
+    norb = orb.shape[1]
+    pitch = norb + 8
+    rows = norb // SUBS
+    batch = min(4, G)
 
     def peer(i):
         y = (my_y + i // (2 * gx)) % gy
@@ -287,13 +296,13 @@
         block = held[k]
 
         def some(t, c):
-            for i in range(4):
-                g = t * 4 + i
+            for i in range(batch):
+                g = t * batch + i
                 for s in range(4):
-                    send[k, g, s] = block[lists[(g * 8 + p) * 4 + s]]
-            return c
-
-        lax.fori_loop(0, G // 4, some, 0)
+                    send[k, g, s] = block[lists[p, s, g]]
+            return c
+
+        lax.fori_loop(0, G // batch, some, 0)
 
     def push(k):
         def one(i, c):
@@ -306,6 +315,20 @@
         pltpu.make_async_copy(send.at[k, me], land.at[k, me], rsem.at[k]).start()
         lax.fori_loop(1, G, one, 0)
 
+    for jj in range(2):
+        for half in range(2):
+            for xx in range(2):
+                r = 4 * jj + 2 * half + xx
+                lane = jj * 256 + half * 128
+                wide[r * pitch:r * pitch + norb, :] = orb[xx, :, lane:lane + 128].astype(f32)
+
+    def regroup(t, c):
+        for i in range(8):
+            o = t * 8 + i
+            held[0][o] = wide[pl.ds(o, 8, stride=pitch), :].astype(bf16)
+        return c
+
+    lax.fori_loop(0, norb // 8, regroup, 0)
     pick(0)
     pl.semaphore_wait(barrier, G + 1)
     for sub in range(SUBS):
@@ -336,36 +359,208 @@
 
 def gather_boxes(orb, lists, gy, gx):
     G = gy * gx * 2
-    norb = orb.shape[0]
+    norb = orb.shape[1]
     vmem = pl.BlockSpec(memory_space=pltpu.VMEM)
     return pl.pallas_call(
         lambda *refs: gather_kernel(gy, gx, *refs),
         out_shape=jax.ShapeDtypeStruct((8, G, 4, 8, 128), bf16),
         in_specs=[vmem, pl.BlockSpec(memory_space=pltpu.SMEM)],
         out_specs=vmem,
-        scratch_shapes=[pltpu.VMEM((norb, 8, 128), bf16)] * 7 + [
+        scratch_shapes=[pltpu.VMEM((norb, 8, 128), bf16)] * 8 + [
+            pltpu.VMEM((8 * (norb + 8), 128), f32),
             pltpu.VMEM((8, G, 4, 8, 128), bf16),
             pltpu.SemaphoreType.DMA((2, 4, SUBS)),
             pltpu.SemaphoreType.DMA((2, 4, SUBS)),
             pltpu.SemaphoreType.DMA((8,)),
             pltpu.SemaphoreType.DMA((8,)),
         ],
-        compiler_params=pltpu.CompilerParams(collective_id=0, has_side_effects=True, vmem_limit_bytes=24 << 20),
+        compiler_params=pltpu.CompilerParams(collective_id=0, has_side_effects=True, vmem_limit_bytes=12 << 20),
         name="gather_boxes",
     )(orb, lists)
 
 
+ORDER = ((4, None), (3, None), (5, None), (2, None), (6, None), (1, None), (7, None), (0, None))
+NF, NS = 3, 5
+
+
+def collect_kernel(gy, gx, norb, fields, lists, out, keys, rows, bufa, bufb, bufc, bufd, sumc, sumd, hot, hotc,
+                   ssem, rsem, zsend, zrecv):
+    G = gy * gx * 2
+    HG = G // 2
+    K = G * 16
+    R = 4 * norb
+    me = lax.axis_index("grid")
+    p = lax.axis_index("pair")
+    my_y, my_x, my_c = me // (2 * gx), (me // 2) % gx, me % 2
+    toward = ((p + 1) % 8, (p + 7) % 8)
+
+    def peer(i):
+        y = (my_y + i // (2 * gx)) % gy
+        x = (my_x + (i // 2) % gx) % gx
+        c = (my_c + i) % 2
+        return (y * gx + x) * 2 + c
+
+    barrier = pltpu.get_barrier_semaphore()
+    for z in toward:
+        pl.semaphore_signal(barrier, inc=1, device_id=(me, z), device_id_type=MESH)
+
+    def greet(i, c):
+        pl.semaphore_signal(barrier, inc=1, device_id=(peer(i), p), device_id_type=MESH)
+        return c
+
+    lax.fori_loop(1, G, greet, 0)
+
+    col_g = lax.broadcasted_iota(jnp.int32, (G, K), 1)
+    row_g = lax.broadcasted_iota(jnp.int32, (G, K), 0)
+    all_keys = ((lax.broadcasted_iota(jnp.int32, (8, K), 1) % 4) * norb).astype(f32)
+    for s in range(4):
+        pattern = (col_g // 16 == row_g) & (col_g // 4 % 4 == s)
+        pattern = jnp.where(pattern, jnp.float32(1), jnp.float32(0)).astype(bf16)
+        all_keys = all_keys + mm(lists[:, s, :].astype(f32).astype(bf16), pattern)
+    keys[...] = all_keys.astype(jnp.int32)
+
+    def choose(q, lo, n):
+        key = keys[pl.ds(q, 1), lo:lo + n]
+        rowid = lax.broadcasted_iota(jnp.int32, (R, n), 0)
+        return jnp.where(rowid == key, jnp.float32(1), jnp.float32(0)).astype(bf16)
+
+    hot[...] = choose(p, 0, K)
+    pl.semaphore_wait(barrier, G + 1)
+
+    def view(ref, k, g, h):
+        return ref.at[k, g] if h is None else ref.at[k, g, h]
+
+    def slot(k, h):
+        return k
+
+    def spread(k, h=None):
+        sem = slot(k, h)
+        pltpu.make_async_copy(view(fields, k, me, h), view(rows, k, me, h), rsem.at[sem]).start()
+
+        def push(i, c):
+            g = peer(i)
+            pltpu.make_async_remote_copy(
+                src_ref=view(fields, k, g, h), dst_ref=view(rows, k, me, h), send_sem=ssem.at[sem],
+                recv_sem=rsem.at[sem], device_id=(g, p), device_id_type=MESH).start()
+            return c
+
+        lax.fori_loop(1, G, push, 0)
+
+    def landed(k, h=None):
+        part = view(rows, k, slice(None), h)
+        pltpu.make_async_copy(part, part, rsem.at[slot(k, h)]).wait()
+
+    def hop(d, stage, h):
+        if stage == 0:
+            src, dst = rows.at[4, pl.ds(d * HG, HG), h], bufa.at[d, h]
+        elif stage == 1:
+            src, dst = rows.at[(3, 5)[d], :, h], bufb.at[d, h, pl.ds(0, G)]
+        elif stage == 2:
+            src, dst = bufa.at[d, h], bufb.at[d, h, pl.ds(G, HG)]
+        elif stage == 3:
+            src, dst = sumc.at[d, h], bufc.at[d, h]
+        else:
+            src, dst = sumd.at[d, h], bufd.at[d, h]
+        return pltpu.make_async_remote_copy(
+            src_ref=src, dst_ref=dst, send_sem=zsend.at[d, stage, h], recv_sem=zrecv.at[d, stage, h],
+            device_id=(me, toward[d]), device_id_type=MESH)
+
+    def own(k, h):
+        return mm(hot[...], rows[k, :, h].reshape(K, 128))
+
+    for k, h in ORDER[:NF]:
+        spread(k, h)
+    landed(4)
+    for h in range(2):
+        for d in range(2):
+            hop(d, 0, h).start()
+    for k, h in ORDER[NF:NS]:
+        spread(k, h)
+    for d in range(2):
+        q1, q2 = ((p + 7) % 8, (p + 6) % 8) if d == 0 else ((p + 1) % 8, (p + 2) % 8)
+        hotc[d, :, 0:K] = choose(q1, 0, K)
+        hotc[d, :, K:K + K // 2] = choose(q2, d * (K // 2), K // 2)
+    for h in range(2):
+        for d in range(2):
+            if h == 0:
+                landed((3, 5)[d])
+            hop(d, 1, h).start()
+            hop(d, 0, h).wait_recv()
+            hop(d, 2, h).start()
+    for k, h in ORDER[NS:]:
+        spread(k, h)
+    landed(2)
+    landed(6)
+    for h in range(2):
+        for d in range(2):
+            hop(d, 1, h).wait_recv()
+            hop(d, 2, h).wait_recv()
+            sumc[d, h] = own((2, 6)[d], h) + mm(hotc[d], bufb[d, h].reshape(K + K // 2, 128))
+            hop(d, 3, h).start()
+    landed(1)
+    landed(7)
+    landed(0)
+    mine = [own(0, h) for h in range(2)]
+    for h in range(2):
+        for d in range(2):
+            part = own((1, 7)[d], h)
+            hop(d, 3, h).wait_recv()
+            sumd[d, h] = (part + bufc[d, h]).astype(bf16)
+            hop(d, 4, h).start()
+    for h in range(2):
+        for d in range(2):
+            hop(d, 4, h).wait_recv()
+        total = mine[h] + bufd[0, h].astype(f32) + bufd[1, h].astype(f32)
+        for jj in range(2):
+            for xx in range(2):
+                i = jj * 2 + xx
+                out[xx, :, jj * 256 + h * 128:jj * 256 + (h + 1) * 128] = total[i * norb:(i + 1) * norb]
+    for d in range(2):
+        for stage in range(5):
+            for h in range(2):
+                hop(d, stage, h).wait_send()
+    for k, h in ORDER:
+        many = pl.ds(1, G - 1)
+        pltpu.make_async_remote_copy(
+            src_ref=view(fields, k, many, h), dst_ref=view(rows, k, many, h), send_sem=ssem.at[slot(k, h)],
+            recv_sem=rsem.at[slot(k, h)], device_id=(me, toward[0]), device_id_type=MESH).wait_send()
+
+
+def collect_fields(fields, lists, norb, gy, gx):
+    G = gy * gx * 2
+    vmem = pl.BlockSpec(memory_space=pltpu.VMEM)
+    sums = pltpu.VMEM((2, 2, 4 * norb, 128), f32)
+    last = pltpu.VMEM((2, 2, 4 * norb, 128), bf16)
+    return pl.pallas_call(
+        lambda *refs: collect_kernel(gy, gx, norb, *refs),
+        out_shape=jax.ShapeDtypeStruct((2, norb, 512), f32),
+        in_specs=[vmem, vmem],
+        out_specs=vmem,
+        scratch_shapes=[
+            pltpu.VMEM((8, G * 16), jnp.int32),
+            pltpu.VMEM((8, G, 2, 16, 128), bf16),
+            pltpu.VMEM((2, 2, G // 2, 16, 128), bf16),
+            pltpu.VMEM((2, 2, G + G // 2, 16, 128), bf16),
+            sums, last, sums, last,
+            pltpu.VMEM((4 * norb, G * 16), bf16),
+            pltpu.VMEM((2, 4 * norb, G * 24), bf16),
+            pltpu.SemaphoreType.DMA((10,)),
+            pltpu.SemaphoreType.DMA((10,)),
+            pltpu.SemaphoreType.DMA((2, 5, 2)),
+            pltpu.SemaphoreType.DMA((2, 5, 2)),
+        ],
+        compiler_params=pltpu.CompilerParams(collective_id=1, has_side_effects=True, vmem_limit_bytes=18 << 20),
+        name="collect_fields",
+    )(fields, lists)
+
+
 def shards(orbitals, box_list, pair_slots, offsets, pair_count):
-    planes, orbital_total, row_cells = orbitals.shape
-    lists = box_list.reshape(-1)
-    orb = orbitals.reshape(planes, orbital_total, 4, 128).transpose(1, 2, 0, 3).reshape(orbital_total, 8, 128)
-    land = gather_boxes(orb, lists, 4, 4)
-    back = worker_fields(land, pair_slots[0, 0], offsets[0, 0], pair_count[0])
-    landed = lax.all_to_all(back.reshape(256, 4, 8, 128), ("grid", "pair"), split_axis=0, concat_axis=0, tiled=True)
-    hot = (lists[:, None] == jnp.arange(orbital_total, dtype=jnp.int32)[None, :]).astype(bf16)
-    landed = landed.reshape(1024, 4, planes, 128)
-    summed = jnp.einsum("ro,rqxc->xoqc", hot, landed, preferred_element_type=f32)
-    return summed.reshape(planes, orbital_total, row_cells)
+    lists = jnp.transpose(box_list, (1, 2, 0))
+    slots = jnp.transpose(pair_slots, (0, 1, 3, 2)).reshape(2, 4)
+    offs = jnp.transpose(offsets, (0, 3, 1, 2)).reshape(3, 1, 4)
+    land = gather_boxes(orbitals, lists, 4, 4)
+    fields = worker_fields(land, slots, offs, pair_count)
+    return collect_fields(fields, lists, orbitals.shape[1], 4, 4)
 
 
 def solution(mesh):

time: 139 us -> 116 us (0.83)
  blocking collectives: 66.6 us -> 0 us
  Pallas kernels: 65 us -> 113 us
  local copies, waits for them, and re-layouts: 4.97 us -> 2.48 us
    all_to_all x1 -> x0, blocking collectives: 66.6 us -> none  [shards(): lax.all_to_all(back.reshape(256, 4, 8, 128), ('grid', 'pair'), split_axis...]
    pallas_call x1 -> x2, Pallas kernels: 21.5 us -> 68.9 us  [the longest x1 48.4 us: collect_fields(): pl.pallas_call(lambda *refs: collect_kernel(gy, gx, norb, *refs), out_sha...]
    reshape x4 -> x0, local copies, waits for them, and re-layouts: 2.54 us -> none  [the longest x2 1.42 us: shards(): orbitals.reshape(planes, orbital_total, 4, 128).transpose(1, 2, 0, 3)]
where the time goes in v4:
time: 116 us
  Pallas kernels  113 us (97%)
  local copies, waits for them, and re-layouts  2.48 us (2%)
    pallas_call x1, Pallas kernels, collect_fields(): pl.pallas_call(lambda *refs: collect_kernel(gy, gx, norb, *refs), out_sha...  48.4 us
    pallas_call x1, Pallas kernels, gather_boxes(): pl.pallas_call(lambda *refs: gather_kernel(gy, gx, *refs), out_shape=jax....  43.8 us
    pallas_call x1, Pallas kernels, worker_fields(): pl.pallas_call(pair_kernel, out_shape=jax.ShapeDtypeStruct((8, 32, 2, 16,...  20.6 us
    unnamed x19, local copies, waits for them, and re-layouts  2.48 us

profile of v4, /device:TPU:1, one launch (start us, length us, event | category | flops | bytes accessed | tf_op | source)
XLA Modules:
  0.0 116.1 jit_solution(6678767065419099258)
XLA Ops:
  0.0 0.0 copy-start
  0.0 0.0 copy-start.1
  0.8 0.0 copy-start.2
  0.8 0.9 copy-done.2
  1.7 0.0 copy-start.3
  1.7 0.7 copy-done.3
  2.4 0.0 copy-start.5
  2.4 0.0 copy-start.6
  2.4 0.0 copy-start.7
  2.4 0.0 copy-start.8
  2.4 43.8 %gather_boxes.1.land = bf16[8,32,4,8,128]{4,3,2,1,0:T(8,128)(2,1)S(1)} custom-call(bf16[2,128,512]{2,1,0:T(8,128)(2,1)S(1)} %copy-done.2, s32[8,4,32]{2,1,0:T(4,128)S(1)} %bitcast.7), custom_call_target="tpu_custom_call" | custom-call | tf_op jit(solution)/shard_map/gather_boxes/pallas_call | solution.py:364
  46.3 0.0 copy-done
  46.3 0.0 copy-done.1
  46.3 0.0 copy-done.5
  46.3 0.0 copy-done.6
  46.3 0.0 copy-done.7
  46.3 0.0 copy-done.8
  46.3 0.0 copy-start.4
  46.3 20.6 %pairs.1.refs_0_ = bf16[8,32,2,16,128]{4,3,2,1,0:T(8,128)(2,1)S(1)} custom-call(s32[2,4]{1,0:T(2,128)S(1)} %bitcast.10, s32[3,1,4]{2,1,0:T(1,128)S(1)} %bitcast.9, s32[1,1]{1,0:T(1,128)S(6)} %copy.11.count, bf16[8,32,4,8,128]{4,3,2,1,0:T(8,128)(2,1)S(1)} %gather_boxes.1.land, bf16[64,192]{1,0:T(8,128)(2,1)S(1)} %copy-done.6, bf16[64,192]{1,0:T(8,128)(2,1)S(1)} %copy-done.5, ...), custom_call_target="tpu_custom_call" | custom-call | tf_op jit(solution)/shard_map/pairs/pallas_call | solution.py:230
  66.9 0.0 copy-done.4
  66.9 48.4 %collect_fields.1 = f32[2,128,512]{2,1,0:T(8,128)S(1)} custom-call(bf16[8,32,2,16,128]{4,3,2,1,0:T(8,128)(2,1)S(1)} %pairs.1.refs_0_, s32[8,4,32]{2,1,0:T(4,128)S(1)} %bitcast.8), custom_call_target="tpu_custom_call" | custom-call | tf_op jit(solution)/shard_map/collect_fields/pallas_call | solution.py:534
  115.3 0.8 copy.12
Async XLA Ops:
  0.0 46.3 %copy-start = (f32[16,64,256]{2,1,0:T(8,128)S(1)}, f32[16,64,256]{2,1,0:T(8,128)}, u32[]{:S(2)}) copy-start(f32[16,64,256]{2,1,0:T(8,128)} %constant.11.clone.green) | copy-start | bytes 3145732
  0.0 46.3 %copy-start.1 = (bf16[768,256]{1,0:T(8,128)(2,1)S(1)}, bf16[768,256]{1,0:T(8,128)(2,1)}, u32[]{:S(2)}) copy-start(bf16[768,256]{1,0:T(8,128)(2,1)} %constant.10.clone.bd) | copy-start | bytes 1179652
  0.8 1.0 copy-start.2
  1.7 0.7 copy-start.3
  2.4 43.8 %copy-start.5 = (bf16[64,192]{1,0:T(8,128)(2,1)S(1)}, bf16[64,192]{1,0:T(8,128)(2,1)}, u32[]{:S(2)}) copy-start(bf16[64,192]{1,0:T(8,128)(2,1)} %constant.9.clone.ux) | copy-start | bytes 73732
  2.4 43.8 %copy-start.6 = (bf16[64,192]{1,0:T(8,128)(2,1)S(1)}, bf16[64,192]{1,0:T(8,128)(2,1)}, u32[]{:S(2)}) copy-start(bf16[64,192]{1,0:T(8,128)(2,1)} %constant.8.clone.cx) | copy-start | bytes 73732
  2.4 43.9 %copy-start.7 = (s32[1,1,4,3]{2,1,3,0:T(1,128)S(1)}, s32[1,1,4,3]{2,1,3,0:T(1,128)}, u32[]{:S(2)}) copy-start(s32[1,1,4,3]{2,1,3,0:T(1,128)} %param.12) | copy-start | bytes 148
  2.4 43.9 %copy-start.8 = (s32[1,1,4,2]{2,3,1,0:T(2,128)S(1)}, s32[1,1,4,2]{2,3,1,0:T(2,128)}, u32[]{:S(2)}) copy-start(s32[1,1,4,2]{2,3,1,0:T(2,128)} %param.11) | copy-start | bytes 100
  46.3 20.6 %copy-start.4 = (s32[32,8,4]{0,2,1:T(4,128)S(1)}, s32[32,8,4]{0,2,1:T(4,128)}, u32[]{:S(2)}) copy-start(s32[32,8,4]{0,2,1:T(4,128)} %param.10) | copy-start | bytes 12292

commit v5 on v4

--- a/solution.py
+++ b/solution.py
@@ -11,8 +11,8 @@
 N = 64
 CH = 16
 W = 256
-PITCH = 72
-PITCH2 = 24
+PITCH = 68
+PITCH2 = 20
 f32, bf16 = jnp.float32, jnp.bfloat16
 
 
@@ -64,15 +64,14 @@
     return mm(jnp.concatenate([hi, lo, hi], axis=1), bd)
 
 
-def pair_kernel(slots, offs, count, land, cx, ux, bd, green, out, box, pad, X, U, F, wh, wl, col):
-    GR = 16
+def pair_kernel(slots, offs, count, land, cx, ux, bd, green, out, box, S, SH, U, F, col):
     low = lax.broadcasted_iota(jnp.int32, (32, 128), 1) < 64
-    zpad = jnp.zeros((4, N, W), bf16)
-    for r in (pad, wh, wl):
-        r[0:4] = zpad
-        r[20:24] = zpad
+    lane = lax.broadcasted_iota(jnp.int32, (N, 128), 1)
+    for r in (slice(0, 6), slice(38, 44)):
+        S[r] = jnp.zeros((6, 96, 128), f32)
+    for r in (0, 40, 48, 88):
+        S[6:38, r:r + 8, :] = jnp.zeros((32, 8, 128), f32)
     col[...] = jnp.zeros(col.shape, f32)
-    X[...] = jnp.zeros(X.shape, f32)
     place = lax.axis_index("pair")
 
     def arrange(s, c):
@@ -80,7 +79,7 @@
             for i in range(4):
                 g = t * 4 + i
                 for k in range(8):
-                    F[pl.ds(pl.multiple_of(g * PITCH, 8) + 8 * k, 8), :] = land[k, g, s].astype(f32)
+                    F[pl.ds(pl.multiple_of(g * PITCH, 4) + 8 * k, 8), :] = land[k, g, s].astype(f32)
             return c2
 
         lax.fori_loop(0, 8, widen, 0)
@@ -99,58 +98,41 @@
         b = slots[1, k]
         dx, dy, dz = offs[0, 0, k], offs[1, 0, k], offs[2, 0, k]
         t = dy * 64 + dz
-        q = (t + 1024) // 256 - 4
-        r = t - 256 * q
-        rows = lax.broadcasted_iota(jnp.int32, (W, W), 0)
-        cols = lax.broadcasted_iota(jnp.int32, (W, W), 1)
-        zc = cols % 64 + dz
-        okc = (zc >= 0) & (zc < 64)
-        one, zero = jnp.float32(1), jnp.float32(0)
-
-        def mask(c):
-            return jnp.where(c, one, zero).astype(bf16)
-
-        fwd = jnp.concatenate([mask(okc & (rows == cols + r)), mask(okc & (rows == cols + r - 256))], axis=0)
-        zr = rows % 64 + dz
-        okr = (zr >= 0) & (zr < 64)
-        b0 = mask(okr & (cols == rows + r))
-        b1 = mask(okr & (cols == rows + r - 256))
-        bwd = jnp.concatenate([b0, b0, b1, b1], axis=0)
-        pad[4:20] = box[b]
+        q = (t + 1024) // 128 - 8
+        r = t - 128 * q
+        z = lane % 64
+        inside = (z + dz >= 0) & (z + dz < 64)
+        inside_back = (z - dz >= 0) & (z - dz < 64)
 
         def put(j, v):
             for h in range(2):
                 for e in range(2):
-                    X[j, h, e * 48 + 8:e * 48 + 40, :] = v[e * 32:(e + 1) * 32, h * 128:(h + 1) * 128]
-
-        def moved(j, step):
-            halves = []
+                    S[6 + 2 * j + h, e * 48 + 8:e * 48 + 40, :] = v[e * 32:(e + 1) * 32, h * 128:(h + 1) * 128]
+
+        def fetch(tile, step, turn):
+            both = []
+            for e in range(2):
+                n = step + 16 + e
+                both.append(S[tile, pl.ds(n % 2 * 48 + n // 2, 32), :])
+            return pltpu.roll(jnp.concatenate(both, axis=0), turn, 1)
+
+        for j in range(CH):
+            put(j, box[b, j].astype(f32))
+        turn = (128 - r) % 128
+        here = fetch(6 + q, dx, turn)
+        for T in range(2 * CH):
+            then = fetch(7 + T + q, dx, turn)
+            SH[T] = jnp.where(inside, jnp.where(lane < 128 - r, here, then), jnp.float32(0))
+            here = then
+
+        outs = []
+        for j in range(CH):
+            moved = jnp.concatenate([SH[2 * j], SH[2 * j + 1]], axis=1)
+            outs.append(left_mul(cx[...], box[a, j].astype(f32) * moved))
+        spec = right_mul(jnp.concatenate(outs, axis=0), bd[...])
+        for j in range(CH):
             for h in range(2):
-                both = []
-                for e in range(2):
-                    n = step + 16 + e
-                    both.append(X[j, h, pl.ds(n % 2 * 48 + n // 2, 32), :])
-                halves.append(jnp.concatenate(both, axis=0))
-            return jnp.concatenate(halves, axis=1)
-
-        def forward(g, c):
-            lo_ = g * GR
-            src0 = pad[pl.ds(lo_ + 4 + q, GR)].reshape(GR * N, W)
-            src1 = pad[pl.ds(lo_ + 5 + q, GR)].reshape(GR * N, W)
-            yz = mm(jnp.concatenate([src0, src1], axis=1), fwd).reshape(GR, N, W)
-            for i in range(GR):
-                put(lo_ + i, yz[i])
-            outs = []
-            for i in range(GR):
-                dens = box[a, lo_ + i].astype(f32) * moved(lo_ + i, dx)
-                outs.append(left_mul(cx[...], dens))
-            spec = right_mul(jnp.concatenate(outs, axis=0), bd[...])
-            for i in range(GR):
-                for h in range(2):
-                    U[pl.ds(pl.multiple_of((2 * (lo_ + i) + h) * PITCH, 8), N), :] = spec[i * N:(i + 1) * N, h * 128:(h + 1) * 128]
-            return c
-
-        lax.fori_loop(0, CH // GR, forward, 0)
+                U[(2 * j + h) * PITCH:(2 * j + h) * PITCH + N, :] = spec[j * N:(j + 1) * N, h * 128:(h + 1) * 128]
 
         def middle(g, c):
             tops, bots = [], []
@@ -171,32 +153,23 @@
 
         lax.fori_loop(0, CH, middle, 0, unroll=8)
 
-        def inverse(g, c):
-            lo_ = g * GR
-            outs = []
-            for i in range(GR):
-                v = jnp.concatenate(
-                    [U[pl.ds(pl.multiple_of((2 * (lo_ + i) + h) * PITCH, 8), N), :] for h in range(2)], axis=1)
-                outs.append(left_mul(ux[...], v))
-            pot = right_mul(jnp.concatenate(outs, axis=0), bd[...]).reshape(GR, N, W)
-            for i in range(GR):
-                j = lo_ + i
-                col[a, j] = col[a, j] - pot[i] * moved(j, dx)
-                put(j, -(pot[i] * box[a, j].astype(f32)))
-                wh[j + 4], wl[j + 4] = split(moved(j, -dx))
-            return c
-
-        lax.fori_loop(0, CH // GR, inverse, 0)
-
-        def back(g, c):
-            lo_ = g * GR
-            i0 = lo_ + 4 - q
-            parts_ = [r_[pl.ds(i, GR)].reshape(GR * N, W) for i in (i0, i0 - 1) for r_ in (wh, wl)]
-            u = mm(jnp.concatenate(parts_, axis=1), bwd)
-            col[b, pl.ds(lo_, GR)] = col[b, pl.ds(lo_, GR)] + u.reshape(GR, N, W)
-            return c
-
-        lax.fori_loop(0, CH // GR, back, 0)
+        outs = []
+        for j in range(CH):
+            v = jnp.concatenate([U[(2 * j + h) * PITCH:(2 * j + h) * PITCH + N, :] for h in range(2)], axis=1)
+            outs.append(left_mul(ux[...], v))
+        pot = right_mul(jnp.concatenate(outs, axis=0), bd[...]).reshape(CH, N, W)
+        for j in range(CH):
+            moved = jnp.concatenate([SH[2 * j], SH[2 * j + 1]], axis=1)
+            col[a, j] = col[a, j] - pot[j] * moved
+            put(j, -(pot[j] * box[a, j].astype(f32)))
+
+        here = fetch(5 - q, -dx, r)
+        for T in range(2 * CH):
+            then = fetch(6 + T - q, -dx, r)
+            u = jnp.where(inside_back, jnp.where(lane < r, here, then), jnp.float32(0))
+            part = slice(T % 2 * 128, T % 2 * 128 + 128)
+            col[b, T // 2, :, part] = col[b, T // 2, :, part] + u
+            here = then
         return carry
 
     lax.fori_loop(0, count[0, 0], pair, 0)
@@ -214,7 +187,7 @@
             for i in range(4):
                 g = t * 4 + i
                 for half in range(2):
-                    out[k, g, half] = F[pl.ds(pl.multiple_of((half * 32 + g) * PITCH2, 8), 16), :].astype(bf16)
+                    out[k, g, half] = F[pl.ds(pl.multiple_of((half * 32 + g) * PITCH2, 4), 16), :].astype(bf16)
             return c2
 
         lax.fori_loop(0, 8, narrow, 0)
@@ -234,12 +207,10 @@
         out_specs=vmem,
         scratch_shapes=[
             pltpu.VMEM((4, CH, N, W), bf16),
-            pltpu.VMEM((24, N, W), bf16),
-            pltpu.VMEM((CH, 2, 96, 128), f32),
+            pltpu.VMEM((44, 96, 128), f32),
+            pltpu.VMEM((2 * CH, N, 128), f32),
             pltpu.VMEM((32 * PITCH, 128), f32),
             pltpu.VMEM((32 * PITCH, 128), f32),
-            pltpu.VMEM((24, N, W), bf16),
-            pltpu.VMEM((24, N, W), bf16),
             pltpu.VMEM((4, CH, N, W), f32),
         ],
         compiler_params=pltpu.CompilerParams(vmem_limit_bytes=28 << 20),
@@ -261,7 +232,7 @@
     right, left = (p + 1) % 8, (p + 7) % 8
     held = blocks
     norb = orb.shape[1]
-    pitch = norb + 8
+    pitch = norb + 4
     rows = norb // SUBS
     batch = min(4, G)
 
@@ -367,7 +338,7 @@
         in_specs=[vmem, pl.BlockSpec(memory_space=pltpu.SMEM)],
         out_specs=vmem,
         scratch_shapes=[pltpu.VMEM((norb, 8, 128), bf16)] * 8 + [
-            pltpu.VMEM((8 * (norb + 8), 128), f32),
+            pltpu.VMEM((8 * (norb + 4), 128), f32),
             pltpu.VMEM((8, G, 4, 8, 128), bf16),
             pltpu.SemaphoreType.DMA((2, 4, SUBS)),
             pltpu.SemaphoreType.DMA((2, 4, SUBS)),

time: 116 us -> 107 us (0.922)
  Pallas kernels: 113 us -> 103 us
    pallas_call x1, Pallas kernels: 20.6 us -> 13.8 us  [worker_fields(): pl.pallas_call(pair_kernel, out_shape=jax.ShapeDtypeStruct((8, 32, 2, 16,...]
    pallas_call x1, Pallas kernels: 48.4 us -> 45.5 us  [collect_fields(): pl.pallas_call(lambda *refs: collect_kernel(gy, gx, norb, *refs), out_sha...]
where the time goes in v5:
time: 107 us; the launch traced here: 106 us
  Pallas kernels  103 us (96%)
  local copies, waits for them, and re-layouts  2.48 us (2%)
    pallas_call x1, Pallas kernels, collect_fields(): pl.pallas_call(lambda *refs: collect_kernel(gy, gx, norb, *refs), out_sha...  45.5 us
    pallas_call x1, Pallas kernels, gather_boxes(): pl.pallas_call(lambda *refs: gather_kernel(gy, gx, *refs), out_shape=jax....  43.8 us
    pallas_call x1, Pallas kernels, worker_fields(): pl.pallas_call(pair_kernel, out_shape=jax.ShapeDtypeStruct((8, 32, 2, 16,...  13.8 us
    unnamed x19, local copies, waits for them, and re-layouts  2.48 us

profile of v5, /device:TPU:1, one launch (start us, length us, event | category | flops | bytes accessed | tf_op | source)
XLA Modules:
  0.0 106.5 jit_solution(12192397997581816976)
XLA Ops:
  0.0 0.0 copy-start
  0.0 0.0 copy-start.1
  0.8 0.0 copy-start.2
  0.8 0.9 copy-done.2
  1.7 0.0 copy-start.3
  1.7 0.7 copy-done.3
  2.4 0.0 copy-start.5
  2.4 0.0 copy-start.6
  2.4 0.0 copy-start.7
  2.4 0.0 copy-start.8
  2.4 43.8 %gather_boxes.1.land = bf16[8,32,4,8,128]{4,3,2,1,0:T(8,128)(2,1)S(1)} custom-call(bf16[2,128,512]{2,1,0:T(8,128)(2,1)S(1)} %copy-done.2, s32[8,4,32]{2,1,0:T(4,128)S(1)} %bitcast.7), custom_call_target="tpu_custom_call" | custom-call | tf_op jit(solution)/shard_map/gather_boxes/pallas_call | solution.py:335
  46.3 0.0 copy-done
  46.3 0.0 copy-done.1
  46.3 0.0 copy-done.5
  46.3 0.0 copy-done.6
  46.3 0.0 copy-done.7
  46.3 0.0 copy-done.8
  46.3 0.0 copy-start.4
  46.3 13.8 %pairs.1.refs_0_ = bf16[8,32,2,16,128]{4,3,2,1,0:T(8,128)(2,1)S(1)} custom-call(s32[2,4]{1,0:T(2,128)S(1)} %bitcast.10, s32[3,1,4]{2,1,0:T(1,128)S(1)} %bitcast.9, s32[1,1]{1,0:T(1,128)S(6)} %copy.11.count, bf16[8,32,4,8,128]{4,3,2,1,0:T(8,128)(2,1)S(1)} %gather_boxes.1.land, bf16[64,192]{1,0:T(8,128)(2,1)S(1)} %copy-done.6, bf16[64,192]{1,0:T(8,128)(2,1)S(1)} %copy-done.5, ...), custom_call_target="tpu_custom_call" | custom-call | tf_op jit(solution)/shard_map/pairs/pallas_call | solution.py:203
  60.1 0.0 copy-done.4
  60.1 45.5 %collect_fields.1 = f32[2,128,512]{2,1,0:T(8,128)S(1)} custom-call(bf16[8,32,2,16,128]{4,3,2,1,0:T(8,128)(2,1)S(1)} %pairs.1.refs_0_, s32[8,4,32]{2,1,0:T(4,128)S(1)} %bitcast.8), custom_call_target="tpu_custom_call" | custom-call | tf_op jit(solution)/shard_map/collect_fields/pallas_call | solution.py:505
  105.7 0.8 copy.12
Async XLA Ops:
  0.0 46.3 %copy-start = (f32[16,64,256]{2,1,0:T(8,128)S(1)}, f32[16,64,256]{2,1,0:T(8,128)}, u32[]{:S(2)}) copy-start(f32[16,64,256]{2,1,0:T(8,128)} %constant.11.clone.green) | copy-start | bytes 3145732
  0.0 46.3 %copy-start.1 = (bf16[768,256]{1,0:T(8,128)(2,1)S(1)}, bf16[768,256]{1,0:T(8,128)(2,1)}, u32[]{:S(2)}) copy-start(bf16[768,256]{1,0:T(8,128)(2,1)} %constant.10.clone.bd) | copy-start | bytes 1179652
  0.8 1.0 copy-start.2
  1.7 0.7 copy-start.3
  2.4 43.8 %copy-start.5 = (bf16[64,192]{1,0:T(8,128)(2,1)S(1)}, bf16[64,192]{1,0:T(8,128)(2,1)}, u32[]{:S(2)}) copy-start(bf16[64,192]{1,0:T(8,128)(2,1)} %constant.9.clone.ux) | copy-start | bytes 73732
  2.4 43.8 %copy-start.6 = (bf16[64,192]{1,0:T(8,128)(2,1)S(1)}, bf16[64,192]{1,0:T(8,128)(2,1)}, u32[]{:S(2)}) copy-start(bf16[64,192]{1,0:T(8,128)(2,1)} %constant.8.clone.cx) | copy-start | bytes 73732
  2.4 43.9 %copy-start.7 = (s32[1,1,4,3]{2,1,3,0:T(1,128)S(1)}, s32[1,1,4,3]{2,1,3,0:T(1,128)}, u32[]{:S(2)}) copy-start(s32[1,1,4,3]{2,1,3,0:T(1,128)} %param.12) | copy-start | bytes 148
  2.4 43.9 %copy-start.8 = (s32[1,1,4,2]{2,3,1,0:T(2,128)S(1)}, s32[1,1,4,2]{2,3,1,0:T(2,128)}, u32[]{:S(2)}) copy-start(s32[1,1,4,2]{2,3,1,0:T(2,128)} %param.11) | copy-start | bytes 100
  46.3 13.8 %copy-start.4 = (s32[32,8,4]{0,2,1:T(4,128)S(1)}, s32[32,8,4]{0,2,1:T(4,128)}, u32[]{:S(2)}) copy-start(s32[32,8,4]{0,2,1:T(4,128)} %param.10) | copy-start | bytes 12292

commit v6 on v5

--- a/solution.py
+++ b/solution.py
@@ -13,6 +13,7 @@
 W = 256
 PITCH = 68
 PITCH2 = 20
+PITCH3 = 36
 f32, bf16 = jnp.float32, jnp.bfloat16
 
 
@@ -64,7 +65,7 @@
     return mm(jnp.concatenate([hi, lo, hi], axis=1), bd)
 
 
-def pair_kernel(slots, offs, count, land, cx, ux, bd, green, out, box, S, SH, U, F, col):
+def pair_kernel(slots, offs, count, box, cx, ux, bd, green, col, S, SH, U):
     low = lax.broadcasted_iota(jnp.int32, (32, 128), 1) < 64
     lane = lax.broadcasted_iota(jnp.int32, (N, 128), 1)
     for r in (slice(0, 6), slice(38, 44)):
@@ -72,26 +73,6 @@
     for r in (0, 40, 48, 88):
         S[6:38, r:r + 8, :] = jnp.zeros((32, 8, 128), f32)
     col[...] = jnp.zeros(col.shape, f32)
-    place = lax.axis_index("pair")
-
-    def arrange(s, c):
-        def widen(t, c2):
-            for i in range(4):
-                g = t * 4 + i
-                for k in range(8):
-                    F[pl.ds(pl.multiple_of(g * PITCH, 4) + 8 * k, 8), :] = land[k, g, s].astype(f32)
-            return c2
-
-        lax.fori_loop(0, 8, widen, 0)
-        for k in range(8):
-            j = (place + k) % 8 * 2
-            for jj in range(2):
-                for half in range(2):
-                    two = [F[pl.ds(8 * k + 4 * jj + 2 * half + xx, 32, stride=PITCH), :] for xx in range(2)]
-                    box[s, j + jj, :, half * 128:(half + 1) * 128] = jnp.concatenate(two, axis=0).astype(bf16)
-        return c
-
-    lax.fori_loop(0, 4, arrange, 0)
 
     def pair(k, carry):
         a = slots[0, k]
@@ -174,57 +155,33 @@
 
     lax.fori_loop(0, count[0, 0], pair, 0)
 
-    def deliver(k, c):
-        j = (place + k) % 8 * 2
-        for s in range(4):
-            for jj in range(2):
-                for half in range(2):
-                    for xx in range(2):
-                        F[pl.ds(32 * PITCH2 * half + 4 * s + 2 * jj + xx, 32, stride=PITCH2), :] = (
-                            col[s, j + jj, xx * 32:(xx + 1) * 32, half * 128:(half + 1) * 128])
-
-        def narrow(t, c2):
-            for i in range(4):
-                g = t * 4 + i
-                for half in range(2):
-                    out[k, g, half] = F[pl.ds(pl.multiple_of((half * 32 + g) * PITCH2, 4), 16), :].astype(bf16)
-            return c2
-
-        lax.fori_loop(0, 8, narrow, 0)
-        return c
-
-    lax.fori_loop(0, 8, deliver, 0)
-
-
-def worker_fields(land, slots, offs, count):
+
+def worker_fields(box, slots, offs, count):
     cx, ux, bd, g = (jnp.asarray(t) for t in tables())
     smem = pl.BlockSpec(memory_space=pltpu.SMEM)
     vmem = pl.BlockSpec(memory_space=pltpu.VMEM)
     return pl.pallas_call(
         pair_kernel,
-        out_shape=jax.ShapeDtypeStruct((8, 32, 2, 16, 128), bf16),
+        out_shape=jax.ShapeDtypeStruct((4, CH, N, W), f32),
         in_specs=[smem] * 3 + [vmem] * 5,
         out_specs=vmem,
         scratch_shapes=[
-            pltpu.VMEM((4, CH, N, W), bf16),
             pltpu.VMEM((44, 96, 128), f32),
             pltpu.VMEM((2 * CH, N, 128), f32),
-            pltpu.VMEM((32 * PITCH, 128), f32),
-            pltpu.VMEM((32 * PITCH, 128), f32),
-            pltpu.VMEM((4, CH, N, W), f32),
+            pltpu.VMEM((33 * PITCH, 128), f32),
         ],
         compiler_params=pltpu.CompilerParams(vmem_limit_bytes=28 << 20),
         name="pairs",
-    )(slots, offs, count, land, cx, ux, bd, g)
+    )(slots, offs, count, box, cx, ux, bd, g)
 
 
 MESH = pl.DeviceIdType.MESH
 SUBS = 4
 
 
-def gather_kernel(gy, gx, orb, lists, land, *rest):
+def gather_kernel(gy, gx, orb, lists, box, *rest):
     blocks = rest[:8]
-    wide, send, zsend, zrecv, ssem, rsem = rest[8:]
+    wide, F, land, send, zsend, zrecv, ssem, rsem = rest[8:]
     G = gy * gx * 2
     me = lax.axis_index("grid")
     p = lax.axis_index("pair")
@@ -236,21 +193,25 @@
     rows = norb // SUBS
     batch = min(4, G)
 
-    def peer(i):
-        y = (my_y + i // (2 * gx)) % gy
-        x = (my_x + (i // 2) % gx) % gx
-        c = (my_c + i) % 2
-        return (y * gx + x) * 2 + c
+    across = [((my_x + i // 2) % gx) * 2 + (my_c + i) % 2 for i in range(2 * gx)]
+
+    def each_peer(act):
+        for i in range(1, 2 * gx):
+            act(my_y * (2 * gx) + across[i])
+
+        def line(i, c):
+            y = (my_y + i) % gy * (2 * gx)
+            for a in across:
+                act(y + a)
+            return c
+
+        lax.fori_loop(1, gy, line, 0)
 
     barrier = pltpu.get_barrier_semaphore()
     pl.semaphore_signal(barrier, inc=1, device_id=(me, right), device_id_type=MESH)
     pl.semaphore_signal(barrier, inc=1, device_id=(me, left), device_id_type=MESH)
 
-    def greet(i, c):
-        pl.semaphore_signal(barrier, inc=1, device_id=(peer(i), p), device_id_type=MESH)
-        return c
-
-    lax.fori_loop(1, G, greet, 0)
+    each_peer(lambda g: pl.semaphore_signal(barrier, inc=1, device_id=(g, p), device_id_type=MESH))
 
     def hop(d, h, sub):
         src, dst = (h - 1, h) if d == 0 else ((9 - h) % 8, 8 - h)
@@ -276,15 +237,13 @@
         lax.fori_loop(0, G // batch, some, 0)
 
     def push(k):
-        def one(i, c):
-            g = peer(i)
+        def one(g):
             pltpu.make_async_remote_copy(
                 src_ref=send.at[k, g], dst_ref=land.at[k, me], send_sem=ssem.at[k], recv_sem=rsem.at[k],
                 device_id=(g, p), device_id_type=MESH).start()
-            return c
 
         pltpu.make_async_copy(send.at[k, me], land.at[k, me], rsem.at[k]).start()
-        lax.fori_loop(1, G, one, 0)
+        each_peer(one)
 
     for jj in range(2):
         for half in range(2):
@@ -316,6 +275,25 @@
         for k in (h, 8 - h) if h < 4 else (h,):
             pick(k)
             push(k)
+
+    for k in (0, 1, 7, 2, 6, 3, 5, 4):
+        pltpu.make_async_copy(land.at[k], land.at[k], rsem.at[k]).wait()
+
+        def widen(t, c):
+            for i in range(batch):
+                g = t * batch + i
+                for s in range(4):
+                    F[pl.ds(pl.multiple_of(g * PITCH3, 4) + 8 * s, 8), :] = land[k, g, s].astype(f32)
+            return c
+
+        lax.fori_loop(0, G // batch, widen, 0)
+        j = (p + k) % 8 * 2
+        for s in range(4):
+            for jj in range(2):
+                for half in range(2):
+                    for xx in range(2):
+                        part = F[pl.ds(8 * s + 4 * jj + 2 * half + xx, G, stride=PITCH3), :]
+                        box[s, j + jj, xx * G:(xx + 1) * G, half * 128:(half + 1) * 128] = part.astype(bf16)
     for h in range(1, 5):
         for sub in range(SUBS):
             for d in range(2):
@@ -325,7 +303,6 @@
         pltpu.make_async_remote_copy(
             src_ref=send.at[k, pl.ds(1, G - 1)], dst_ref=land.at[k, pl.ds(1, G - 1)],
             send_sem=ssem.at[k], recv_sem=rsem.at[k], device_id=(me, right), device_id_type=MESH).wait_send()
-        pltpu.make_async_copy(land.at[k], land.at[k], rsem.at[k]).wait()
 
 
 def gather_boxes(orb, lists, gy, gx):
@@ -334,18 +311,20 @@
     vmem = pl.BlockSpec(memory_space=pltpu.VMEM)
     return pl.pallas_call(
         lambda *refs: gather_kernel(gy, gx, *refs),
-        out_shape=jax.ShapeDtypeStruct((8, G, 4, 8, 128), bf16),
+        out_shape=jax.ShapeDtypeStruct((4, 16, 2 * G, 256), bf16),
         in_specs=[vmem, pl.BlockSpec(memory_space=pltpu.SMEM)],
         out_specs=vmem,
         scratch_shapes=[pltpu.VMEM((norb, 8, 128), bf16)] * 8 + [
-            pltpu.VMEM((8 * (norb + 4), 128), f32),
+            pltpu.VMEM((9 * (norb + 4), 128), f32),
+            pltpu.VMEM(((G + 1) * PITCH3, 128), f32),
+            pltpu.VMEM((8, G, 4, 8, 128), bf16),
             pltpu.VMEM((8, G, 4, 8, 128), bf16),
             pltpu.SemaphoreType.DMA((2, 4, SUBS)),
             pltpu.SemaphoreType.DMA((2, 4, SUBS)),
             pltpu.SemaphoreType.DMA((8,)),
             pltpu.SemaphoreType.DMA((8,)),
         ],
-        compiler_params=pltpu.CompilerParams(collective_id=0, has_side_effects=True, vmem_limit_bytes=12 << 20),
+        compiler_params=pltpu.CompilerParams(collective_id=0, has_side_effects=True, vmem_limit_bytes=16 << 20),
         name="gather_boxes",
     )(orb, lists)
 
@@ -354,7 +333,7 @@
 NF, NS = 3, 5
 
 
-def collect_kernel(gy, gx, norb, fields, lists, out, keys, rows, bufa, bufb, bufc, bufd, sumc, sumd, hot, hotc,
+def collect_kernel(gy, gx, norb, col, lists, out, F, fields, keys, rows, bufa, bufb, bufc, bufd, sumc, sumd, hot, hotc,
                    ssem, rsem, zsend, zrecv):
     G = gy * gx * 2
     HG = G // 2
@@ -365,37 +344,52 @@
     my_y, my_x, my_c = me // (2 * gx), (me // 2) % gx, me % 2
     toward = ((p + 1) % 8, (p + 7) % 8)
 
-    def peer(i):
-        y = (my_y + i // (2 * gx)) % gy
-        x = (my_x + (i // 2) % gx) % gx
-        c = (my_c + i) % 2
-        return (y * gx + x) * 2 + c
+    across = [((my_x + i // 2) % gx) * 2 + (my_c + i) % 2 for i in range(2 * gx)]
+
+    def each_peer(act):
+        for i in range(1, 2 * gx):
+            act(my_y * (2 * gx) + across[i])
+
+        def line(i, c):
+            y = (my_y + i) % gy * (2 * gx)
+            for a in across:
+                act(y + a)
+            return c
+
+        lax.fori_loop(1, gy, line, 0)
 
     barrier = pltpu.get_barrier_semaphore()
     for z in toward:
         pl.semaphore_signal(barrier, inc=1, device_id=(me, z), device_id_type=MESH)
 
-    def greet(i, c):
-        pl.semaphore_signal(barrier, inc=1, device_id=(peer(i), p), device_id_type=MESH)
-        return c
-
-    lax.fori_loop(1, G, greet, 0)
-
-    col_g = lax.broadcasted_iota(jnp.int32, (G, K), 1)
-    row_g = lax.broadcasted_iota(jnp.int32, (G, K), 0)
-    all_keys = ((lax.broadcasted_iota(jnp.int32, (8, K), 1) % 4) * norb).astype(f32)
-    for s in range(4):
-        pattern = (col_g // 16 == row_g) & (col_g // 4 % 4 == s)
-        pattern = jnp.where(pattern, jnp.float32(1), jnp.float32(0)).astype(bf16)
-        all_keys = all_keys + mm(lists[:, s, :].astype(f32).astype(bf16), pattern)
-    keys[...] = all_keys.astype(jnp.int32)
+    each_peer(lambda g: pl.semaphore_signal(barrier, inc=1, device_id=(g, p), device_id_type=MESH))
 
     def choose(q, lo, n):
         key = keys[pl.ds(q, 1), lo:lo + n]
         rowid = lax.broadcasted_iota(jnp.int32, (R, n), 0)
         return jnp.where(rowid == key, jnp.float32(1), jnp.float32(0)).astype(bf16)
 
-    hot[...] = choose(p, 0, K)
+    batch = min(4, G)
+
+    def deliver(k):
+        j = (p + k) % 8 * 2
+        for s in range(4):
+            for jj in range(2):
+                for half in range(2):
+                    for xx in range(2):
+                        F[pl.ds(G * PITCH2 * half + 4 * s + 2 * jj + xx, G, stride=PITCH2), :] = (
+                            col[s, j + jj, xx * G:(xx + 1) * G, half * 128:(half + 1) * 128])
+
+        def narrow(t, c):
+            for i in range(batch):
+                g = t * batch + i
+                for half in range(2):
+                    fields[k, g, half] = F[pl.ds(pl.multiple_of((half * G + g) * PITCH2, 4), 16), :].astype(bf16)
+            return c
+
+        lax.fori_loop(0, G // batch, narrow, 0)
+
+    deliver(ORDER[0][0])
     pl.semaphore_wait(barrier, G + 1)
 
     def view(ref, k, g, h):
@@ -408,14 +402,12 @@
         sem = slot(k, h)
         pltpu.make_async_copy(view(fields, k, me, h), view(rows, k, me, h), rsem.at[sem]).start()
 
-        def push(i, c):
-            g = peer(i)
+        def push(g):
             pltpu.make_async_remote_copy(
                 src_ref=view(fields, k, g, h), dst_ref=view(rows, k, me, h), send_sem=ssem.at[sem],
                 recv_sem=rsem.at[sem], device_id=(g, p), device_id_type=MESH).start()
-            return c
-
-        lax.fori_loop(1, G, push, 0)
+
+        each_peer(push)
 
     def landed(k, h=None):
         part = view(rows, k, slice(None), h)
@@ -439,14 +431,28 @@
     def own(k, h):
         return mm(hot[...], rows[k, :, h].reshape(K, 128))
 
-    for k, h in ORDER[:NF]:
-        spread(k, h)
+    def spread_many(lo, hi):
+        for n in range(lo, hi):
+            if n + 1 < len(ORDER):
+                deliver(ORDER[n + 1][0])
+            spread(*ORDER[n])
+
+    spread_many(0, NF)
+    col_g = lax.broadcasted_iota(jnp.int32, (G, K), 1)
+    row_g = lax.broadcasted_iota(jnp.int32, (G, K), 0)
+    all_keys = ((lax.broadcasted_iota(jnp.int32, (8, K), 1) % 4) * norb).astype(f32)
+    for s in range(4):
+        pattern = (col_g // 16 == row_g) & (col_g // 4 % 4 == s)
+        pattern = jnp.where(pattern, jnp.float32(1), jnp.float32(0)).astype(bf16)
+        all_keys = all_keys + mm(lists[:, s, :].astype(f32).astype(bf16), pattern)
+    keys[...] = all_keys.astype(jnp.int32)
+
+    hot[...] = choose(p, 0, K)
     landed(4)
     for h in range(2):
         for d in range(2):
             hop(d, 0, h).start()
-    for k, h in ORDER[NF:NS]:
-        spread(k, h)
+    spread_many(NF, NS)
     for d in range(2):
         q1, q2 = ((p + 7) % 8, (p + 6) % 8) if d == 0 else ((p + 1) % 8, (p + 2) % 8)
         hotc[d, :, 0:K] = choose(q1, 0, K)
@@ -458,8 +464,7 @@
             hop(d, 1, h).start()
             hop(d, 0, h).wait_recv()
             hop(d, 2, h).start()
-    for k, h in ORDER[NS:]:
-        spread(k, h)
+    spread_many(NS, len(ORDER))
     landed(2)
     landed(6)
     for h in range(2):
@@ -497,7 +502,7 @@
             recv_sem=rsem.at[slot(k, h)], device_id=(me, toward[0]), device_id_type=MESH).wait_send()
 
 
-def collect_fields(fields, lists, norb, gy, gx):
+def collect_fields(col, lists, norb, gy, gx):
     G = gy * gx * 2
     vmem = pl.BlockSpec(memory_space=pltpu.VMEM)
     sums = pltpu.VMEM((2, 2, 4 * norb, 128), f32)
@@ -508,6 +513,8 @@
         in_specs=[vmem, vmem],
         out_specs=vmem,
         scratch_shapes=[
+            pltpu.VMEM(((2 * G + 1) * PITCH2, 128), f32),
+            pltpu.VMEM((8, G, 2, 16, 128), bf16),
             pltpu.VMEM((8, G * 16), jnp.int32),
             pltpu.VMEM((8, G, 2, 16, 128), bf16),
             pltpu.VMEM((2, 2, G // 2, 16, 128), bf16),
@@ -520,18 +527,18 @@
             pltpu.SemaphoreType.DMA((2, 5, 2)),
             pltpu.SemaphoreType.DMA((2, 5, 2)),
         ],
-        compiler_params=pltpu.CompilerParams(collective_id=1, has_side_effects=True, vmem_limit_bytes=18 << 20),
+        compiler_params=pltpu.CompilerParams(collective_id=1, has_side_effects=True, vmem_limit_bytes=22 << 20),
         name="collect_fields",
-    )(fields, lists)
+    )(col, lists)
 
 
 def shards(orbitals, box_list, pair_slots, offsets, pair_count):
     lists = jnp.transpose(box_list, (1, 2, 0))
     slots = jnp.transpose(pair_slots, (0, 1, 3, 2)).reshape(2, 4)
     offs = jnp.transpose(offsets, (0, 3, 1, 2)).reshape(3, 1, 4)
-    land = gather_boxes(orbitals, lists, 4, 4)
-    fields = worker_fields(land, slots, offs, pair_count)
-    return collect_fields(fields, lists, orbitals.shape[1], 4, 4)
+    box = gather_boxes(orbitals, lists, 4, 4)
+    col = worker_fields(box, slots, offs, pair_count)
+    return collect_fields(col, lists, orbitals.shape[1], 4, 4)
 
 
 def solution(mesh):

time: 107 us -> 110 us (1.028)
  local copies, waits for them, and re-layouts: 2.48 us -> 7.55 us
    unnamed x19, local copies, waits for them, and re-layouts: 2.48 us -> 7.55 us
    pallas_call x1, Pallas kernels: 45.5 us -> 42.5 us  [collect_fields(): pl.pallas_call(lambda *refs: collect_kernel(gy, gx, norb, *refs), out_sha...]
    pallas_call x1, Pallas kernels: 13.8 us -> 15.9 us  [worker_fields(): pl.pallas_call(pair_kernel, out_shape=jax.ShapeDtypeStruct((4, CH, N, W),...]
where the time goes in v6:
time: 110 us
  Pallas kernels  102 us (93%)
  local copies, waits for them, and re-layouts  7.55 us (7%)
    pallas_call x1, Pallas kernels, gather_boxes(): pl.pallas_call(lambda *refs: gather_kernel(gy, gx, *refs), out_shape=jax....  43 us
    pallas_call x1, Pallas kernels, collect_fields(): pl.pallas_call(lambda *refs: collect_kernel(gy, gx, norb, *refs), out_sha...  42.5 us
    pallas_call x1, Pallas kernels, worker_fields(): pl.pallas_call(pair_kernel, out_shape=jax.ShapeDtypeStruct((4, CH, N, W),...  15.9 us
    unnamed x19, local copies, waits for them, and re-layouts  7.55 us

profile of v6, /device:TPU:1, one launch (start us, length us, event | category | flops | bytes accessed | tf_op | source)
XLA Modules:
  0.0 109.8 jit_solution(17705830698076793941)
XLA Ops:
  0.7 0.0 copy-start.2
  0.7 0.9 copy-done.2
  1.6 0.0 copy-start.3
  1.6 0.7 copy-done.3
  2.3 43.0 %gather_boxes.1.box = bf16[4,16,64,256]{3,2,1,0:T(8,128)(2,1)S(1)} custom-call(bf16[2,128,512]{2,1,0:T(8,128)(2,1)S(1)} %copy-done.2, s32[8,4,32]{2,1,0:T(4,128)S(1)} %bitcast.7), custom_call_target="tpu_custom_call" | custom-call | tf_op jit(solution)/shard_map/gather_boxes/pallas_call | solution.py:312
  45.4 0.0 copy-start
  45.4 1.2 %copy-done = f32[16,64,256]{2,1,0:T(8,128)S(1)} copy-done((f32[16,64,256]{2,1,0:T(8,128)S(1)}, f32[16,64,256]{2,1,0:T(8,128)}, u32[]{:S(2)}) %copy-start) | copy-done | bytes 1048600
  46.6 0.0 copy-start.1
  46.6 1.0 copy-done.1
  47.6 0.0 copy-start.5
  47.6 0.8 copy-done.5
  48.4 0.0 copy-start.6
  48.4 0.8 copy-done.6
  49.1 0.0 copy-start.7
  49.1 0.7 copy-done.7
  49.8 0.0 copy-start.8
  49.8 0.7 copy-done.8
  50.5 0.0 copy-start.4
  50.5 15.9 %pairs.1.refs_0_ = f32[4,16,64,256]{3,2,1,0:T(8,128)S(1)} custom-call(s32[2,4]{1,0:T(2,128)S(1)} %bitcast.10, s32[3,1,4]{2,1,0:T(1,128)S(1)} %bitcast.9, s32[1,1]{1,0:T(1,128)S(6)} %copy.11.count, bf16[4,16,64,256]{3,2,1,0:T(8,128)(2,1)S(1)} %gather_boxes.1.box, bf16[64,192]{1,0:T(8,128)(2,1)S(1)} %copy-done.6, bf16[64,192]{1,0:T(8,128)(2,1)S(1)} %copy-done.5, ...), custom_call_target="tpu_custom_call" | custom-call | tf_op jit(solution)/shard_map/pairs/pallas_call | solution.py:163
  66.4 0.0 copy-done.4
  66.4 42.5 %collect_fields.1 = f32[2,128,512]{2,1,0:T(8,128)S(1)} custom-call(f32[4,16,64,256]{3,2,1,0:T(8,128)S(1)} %pairs.1.refs_0_, s32[8,4,32]{2,1,0:T(4,128)S(1)} %bitcast.8), custom_call_target="tpu_custom_call" | custom-call | tf_op jit(solution)/shard_map/collect_fields/pallas_call | solution.py:510
  109.0 0.8 copy.12
Async XLA Ops:
  0.7 1.0 copy-start.2
  1.6 0.7 copy-start.3
  45.4 1.2 %copy-start = (f32[16,64,256]{2,1,0:T(8,128)S(1)}, f32[16,64,256]{2,1,0:T(8,128)}, u32[]{:S(2)}) copy-start(f32[16,64,256]{2,1,0:T(8,128)} %constant.11.clone.green) | copy-start | bytes 3145732
  46.6 1.0 copy-start.1
  47.6 0.8 copy-start.5
  48.4 0.8 copy-start.6
  49.1 0.7 copy-start.7
  49.8 0.7 copy-start.8
  50.5 16.0 %copy-start.4 = (s32[32,8,4]{0,2,1:T(4,128)S(1)}, s32[32,8,4]{0,2,1:T(4,128)}, u32[]{:S(2)}) copy-start(s32[32,8,4]{0,2,1:T(4,128)} %param.10) | copy-start | bytes 12292

commit v7 on v6

--- a/solution.py
+++ b/solution.py
@@ -325,6 +325,7 @@
             pltpu.SemaphoreType.DMA((8,)),
         ],
         compiler_params=pltpu.CompilerParams(collective_id=0, has_side_effects=True, vmem_limit_bytes=16 << 20),
+        cost_estimate=pl.CostEstimate(flops=20_000_000_000, bytes_accessed=60_000_000, transcendentals=0),
         name="gather_boxes",
     )(orb, lists)
 

time: 110 us -> 104 us (0.945)
  local copies, waits for them, and re-layouts: 7.55 us -> 2.49 us
    unnamed x19, local copies, waits for them, and re-layouts: 7.55 us -> 2.49 us
where the time goes in v7:
time: 104 us
  Pallas kernels  101 us (97%)
  local copies, waits for them, and re-layouts  2.49 us (2%)
    pallas_call x1, Pallas kernels, gather_boxes(): pl.pallas_call(lambda *refs: gather_kernel(gy, gx, *refs), out_shape=jax....  43.2 us
    pallas_call x1, Pallas kernels, collect_fields(): pl.pallas_call(lambda *refs: collect_kernel(gy, gx, norb, *refs), out_sha...  41.9 us
    pallas_call x1, Pallas kernels, worker_fields(): pl.pallas_call(pair_kernel, out_shape=jax.ShapeDtypeStruct((4, CH, N, W),...  16 us
    unnamed x19, local copies, waits for them, and re-layouts  2.49 us

profile of v7, /device:TPU:1, one launch (start us, length us, event | category | flops | bytes accessed | tf_op | source)
XLA Modules:
  0.0 104.3 jit_solution(13319392788889955914)
XLA Ops:
  0.7 0.0 copy-start.4
  0.7 0.7 copy-done.4
  1.4 0.0 copy-start.8
  1.4 0.9 copy-done.8
  2.3 0.0 copy-start
  2.3 0.0 copy-start.1
  2.3 0.0 copy-start.2
  2.3 0.0 copy-start.3
  2.3 0.0 copy-start.6
  2.3 0.0 copy-start.7
  2.4 43.2 %gather_boxes.1.box = bf16[4,16,64,256]{3,2,1,0:T(8,128)(2,1)S(1)} custom-call(bf16[2,128,512]{2,1,0:T(8,128)(2,1)S(1)} %copy-done.8, s32[8,4,32]{2,1,0:T(4,128)S(1)} %bitcast.7), custom_call_target="tpu_custom_call" | custom-call | flops 20000000000 | bytes 60000000 | tf_op jit(solution)/shard_map/gather_boxes/pallas_call | solution.py:312
  45.5 0.0 copy-done
  45.6 0.0 copy-done.1
  45.6 0.0 copy-done.2
  45.6 0.0 copy-done.3
  45.6 0.0 copy-done.6
  45.6 0.0 copy-done.7
  45.6 0.0 copy-start.5
  45.6 16.0 %pairs.1.refs_0_ = f32[4,16,64,256]{3,2,1,0:T(8,128)S(1)} custom-call(s32[2,4]{1,0:T(2,128)S(1)} %bitcast.10, s32[3,1,4]{2,1,0:T(1,128)S(1)} %bitcast.9, s32[1,1]{1,0:T(1,128)S(6)} %copy.11.count, bf16[4,16,64,256]{3,2,1,0:T(8,128)(2,1)S(1)} %gather_boxes.1.box, bf16[64,192]{1,0:T(8,128)(2,1)S(1)} %copy-done.3, bf16[64,192]{1,0:T(8,128)(2,1)S(1)} %copy-done.2, ...), custom_call_target="tpu_custom_call" | custom-call | tf_op jit(solution)/shard_map/pairs/pallas_call | solution.py:163
  61.6 0.0 copy-done.5
  61.6 41.9 %collect_fields.1 = f32[2,128,512]{2,1,0:T(8,128)S(1)} custom-call(f32[4,16,64,256]{3,2,1,0:T(8,128)S(1)} %pairs.1.refs_0_, s32[8,4,32]{2,1,0:T(4,128)S(1)} %bitcast.8), custom_call_target="tpu_custom_call" | custom-call | tf_op jit(solution)/shard_map/collect_fields/pallas_call | solution.py:511
  103.5 0.8 copy.12
Async XLA Ops:
  0.7 0.7 copy-start.4
  1.4 0.9 copy-start.8
  2.3 43.2 %copy-start = (f32[16,64,256]{2,1,0:T(8,128)S(1)}, f32[16,64,256]{2,1,0:T(8,128)}, u32[]{:S(2)}) copy-start(f32[16,64,256]{2,1,0:T(8,128)} %constant.11.clone.green) | copy-start | bytes 3145732
  2.3 43.2 %copy-start.1 = (bf16[768,256]{1,0:T(8,128)(2,1)S(1)}, bf16[768,256]{1,0:T(8,128)(2,1)}, u32[]{:S(2)}) copy-start(bf16[768,256]{1,0:T(8,128)(2,1)} %constant.10.clone.bd) | copy-start | bytes 1179652
  2.3 43.2 %copy-start.2 = (bf16[64,192]{1,0:T(8,128)(2,1)S(1)}, bf16[64,192]{1,0:T(8,128)(2,1)}, u32[]{:S(2)}) copy-start(bf16[64,192]{1,0:T(8,128)(2,1)} %constant.9.clone.ux) | copy-start | bytes 73732
  2.3 43.3 %copy-start.3 = (bf16[64,192]{1,0:T(8,128)(2,1)S(1)}, bf16[64,192]{1,0:T(8,128)(2,1)}, u32[]{:S(2)}) copy-start(bf16[64,192]{1,0:T(8,128)(2,1)} %constant.8.clone.cx) | copy-start | bytes 73732
  2.3 43.3 %copy-start.6 = (s32[1,1,4,3]{2,1,3,0:T(1,128)S(1)}, s32[1,1,4,3]{2,1,3,0:T(1,128)}, u32[]{:S(2)}) copy-start(s32[1,1,4,3]{2,1,3,0:T(1,128)} %param.12) | copy-start | bytes 148
  2.3 43.3 %copy-start.7 = (s32[1,1,4,2]{2,3,1,0:T(2,128)S(1)}, s32[1,1,4,2]{2,3,1,0:T(2,128)}, u32[]{:S(2)}) copy-start(s32[1,1,4,2]{2,3,1,0:T(2,128)} %param.11) | copy-start | bytes 100
  45.6 16.0 %copy-start.5 = (s32[32,8,4]{0,2,1:T(4,128)S(1)}, s32[32,8,4]{0,2,1:T(4,128)}, u32[]{:S(2)}) copy-start(s32[32,8,4]{0,2,1:T(4,128)} %param.10) | copy-start | bytes 12292

commit v8 on v7

--- a/solution.py
+++ b/solution.py
@@ -176,7 +176,7 @@
 
 
 MESH = pl.DeviceIdType.MESH
-SUBS = 4
+SUBS = 2
 
 
 def gather_kernel(gy, gx, orb, lists, box, *rest):

time: 104 us -> 104 us (level)
    pallas_call x1, Pallas kernels: 41.9 us -> 45.8 us  [collect_fields(): pl.pallas_call(lambda *refs: collect_kernel(gy, gx, norb, *refs), out_sha...]
    pallas_call x1, Pallas kernels: 16 us -> 12.2 us  [worker_fields(): pl.pallas_call(pair_kernel, out_shape=jax.ShapeDtypeStruct((4, CH, N, W),...]
where the time goes in v8:
time: 104 us
  Pallas kernels  101 us (97%)
  local copies, waits for them, and re-layouts  2.49 us (2%)
    pallas_call x1, Pallas kernels, collect_fields(): pl.pallas_call(lambda *refs: collect_kernel(gy, gx, norb, *refs), out_sha...  45.8 us
    pallas_call x1, Pallas kernels, gather_boxes(): pl.pallas_call(lambda *refs: gather_kernel(gy, gx, *refs), out_shape=jax....  42.9 us
    pallas_call x1, Pallas kernels, worker_fields(): pl.pallas_call(pair_kernel, out_shape=jax.ShapeDtypeStruct((4, CH, N, W),...  12.2 us
    unnamed x19, local copies, waits for them, and re-layouts  2.49 us

profile of v8, /device:TPU:1, one launch (start us, length us, event | category | flops | bytes accessed | tf_op | source)
XLA Modules:
  0.0 104.2 jit_solution(11009121836483167191)
XLA Ops:
  0.7 0.0 copy-start.4
  0.7 0.7 copy-done.4
  1.4 0.0 copy-start.8
  1.4 0.9 copy-done.8
  2.3 0.0 copy-start
  2.3 0.0 copy-start.1
  2.3 0.0 copy-start.2
  2.3 0.0 copy-start.3
  2.3 0.0 copy-start.6
  2.3 0.0 copy-start.7
  2.4 42.9 %gather_boxes.1.box = bf16[4,16,64,256]{3,2,1,0:T(8,128)(2,1)S(1)} custom-call(bf16[2,128,512]{2,1,0:T(8,128)(2,1)S(1)} %copy-done.8, s32[8,4,32]{2,1,0:T(4,128)S(1)} %bitcast.7), custom_call_target="tpu_custom_call" | custom-call | flops 20000000000 | bytes 60000000 | tf_op jit(solution)/shard_map/gather_boxes/pallas_call | solution.py:312
  45.2 0.0 copy-done
  45.2 0.0 copy-done.1
  45.3 0.0 copy-done.2
  45.3 0.0 copy-done.3
  45.3 0.0 copy-done.6
  45.3 0.0 copy-done.7
  45.3 0.0 copy-start.5
  45.3 12.2 %pairs.1.refs_0_ = f32[4,16,64,256]{3,2,1,0:T(8,128)S(1)} custom-call(s32[2,4]{1,0:T(2,128)S(1)} %bitcast.10, s32[3,1,4]{2,1,0:T(1,128)S(1)} %bitcast.9, s32[1,1]{1,0:T(1,128)S(6)} %copy.11.count, bf16[4,16,64,256]{3,2,1,0:T(8,128)(2,1)S(1)} %gather_boxes.1.box, bf16[64,192]{1,0:T(8,128)(2,1)S(1)} %copy-done.3, bf16[64,192]{1,0:T(8,128)(2,1)S(1)} %copy-done.2, ...), custom_call_target="tpu_custom_call" | custom-call | tf_op jit(solution)/shard_map/pairs/pallas_call | solution.py:163
  57.5 0.0 copy-done.5
  57.5 45.8 %collect_fields.1 = f32[2,128,512]{2,1,0:T(8,128)S(1)} custom-call(f32[4,16,64,256]{3,2,1,0:T(8,128)S(1)} %pairs.1.refs_0_, s32[8,4,32]{2,1,0:T(4,128)S(1)} %bitcast.8), custom_call_target="tpu_custom_call" | custom-call | tf_op jit(solution)/shard_map/collect_fields/pallas_call | solution.py:511
  103.4 0.8 copy.12
Async XLA Ops:
  0.7 0.7 copy-start.4
  1.4 0.9 copy-start.8
  2.3 42.9 %copy-start = (f32[16,64,256]{2,1,0:T(8,128)S(1)}, f32[16,64,256]{2,1,0:T(8,128)}, u32[]{:S(2)}) copy-start(f32[16,64,256]{2,1,0:T(8,128)} %constant.11.clone.green) | copy-start | bytes 3145732
  2.3 42.9 %copy-start.1 = (bf16[768,256]{1,0:T(8,128)(2,1)S(1)}, bf16[768,256]{1,0:T(8,128)(2,1)}, u32[]{:S(2)}) copy-start(bf16[768,256]{1,0:T(8,128)(2,1)} %constant.10.clone.bd) | copy-start | bytes 1179652
  2.3 42.9 %copy-start.2 = (bf16[64,192]{1,0:T(8,128)(2,1)S(1)}, bf16[64,192]{1,0:T(8,128)(2,1)}, u32[]{:S(2)}) copy-start(bf16[64,192]{1,0:T(8,128)(2,1)} %constant.9.clone.ux) | copy-start | bytes 73732
  2.3 42.9 %copy-start.3 = (bf16[64,192]{1,0:T(8,128)(2,1)S(1)}, bf16[64,192]{1,0:T(8,128)(2,1)}, u32[]{:S(2)}) copy-start(bf16[64,192]{1,0:T(8,128)(2,1)} %constant.8.clone.cx) | copy-start | bytes 73732
  2.3 42.9 %copy-start.6 = (s32[1,1,4,3]{2,1,3,0:T(1,128)S(1)}, s32[1,1,4,3]{2,1,3,0:T(1,128)}, u32[]{:S(2)}) copy-start(s32[1,1,4,3]{2,1,3,0:T(1,128)} %param.12) | copy-start | bytes 148
  2.3 42.9 %copy-start.7 = (s32[1,1,4,2]{2,3,1,0:T(2,128)S(1)}, s32[1,1,4,2]{2,3,1,0:T(2,128)}, u32[]{:S(2)}) copy-start(s32[1,1,4,2]{2,3,1,0:T(2,128)} %param.11) | copy-start | bytes 100
  45.3 12.2 %copy-start.5 = (s32[32,8,4]{0,2,1:T(4,128)S(1)}, s32[32,8,4]{0,2,1:T(4,128)}, u32[]{:S(2)}) copy-start(s32[32,8,4]{0,2,1:T(4,128)} %param.10) | copy-start | bytes 12292
